TPU v7x, 256 devices: a 4x2x16 block of a 4x16x16 slice. The times are simulated.
256 devices in a mesh: rep: 2 (over y), ep: 128 (over x, z, core).
Axes of the slice: x: 4, y: 2, z: 16, core: 2. Of those that a mesh axis runs over, the one named last changes fastest.
The devices are a block of a 4x16x16 slice.
Arguments:
- cache_kv: bfloat16 [512, 2048, 576], P(('rep', 'ep')), parts along dimension 0, may hold values from -6 to 6
- new_kv: bfloat16 [512, 2, 576], P(('rep', 'ep')), parts along dimension 0, may hold values from -6 to 6
- queries: bfloat16 [512, 2, 64, 576], P(('rep', 'ep')), parts along dimension 0, may hold values from -256 to 256
- lengths: int32 [512], P(('rep', 'ep')), parts along dimension 0, may hold values from 256 to 2048
- resid: bfloat16 [512, 2, 7168], P(('rep', 'ep')), parts along dimension 0, may hold values from -18 to 18
- value_up: bfloat16 [512, 8192], P(None, 'ep'), may hold values from -1.5 to 1.5
- out_proj: bfloat16 [8192, 7168], P('ep'), may hold values from -0.09375 to 0.09375
- norm_gain: bfloat16 [7168], replicated, may hold values from 0.25 to 1.75
- router: bfloat16 [7168, 16], replicated, may hold values from -0.0625 to 0.0625
- expert_ids: int32 [512, 2, 8], P(('rep', 'ep')), parts along dimension 0, may hold values from 0 to 15, as said below
- slots: int32 [512, 2, 8], P(('rep', 'ep')), parts along dimension 0, may hold values from 0 to 3, as said below
- w_gate: bfloat16 [7168, 16384], P(None, 'ep'), may hold values from -0.0625 to 0.0625
- w_up: bfloat16 [7168, 16384], P(None, 'ep'), may hold values from -0.0625 to 0.0625
- w_down: bfloat16 [16384, 7168], P('ep'), may hold values from -0.1875 to 0.1875
Outputs:
- mixed: bfloat16 [512, 2, 7168], P(('rep', 'ep')), parts along dimension 0
There are 2 independent parts, one for each index of `rep`. A program takes and returns all parts, laid end to end along the dimension named above; an argument that names none is the same for every part. Nothing has to cross between parts.
Inputs may be any that keep to these rules, and one draw needn't show every extreme that they name: `expert_ids`: each row names 8 different experts. In each aligned block of 4 rows (the rows of one device), the rows that name the same expert carry the distinct slots 0 up to their number minus one for it; in every block some expert is named by all 4 rows.
All inputs are finite; a program needn't handle non-finite values.
Results may differ from a plain program's by a relative error of at most 0.0065.
Values may be sent and summed in bfloat16 or wider, within the bound.
A program may use at most 128 MiB of HBM per device.

v0:
```python
import math

import jax
import jax.numpy as jnp
from jax import lax
from jax.sharding import PartitionSpec as P

D = 7168
H = 64
LAT = 512
VH = 128
EXPERTS = 16
TOP = 8
CAP = 2
QK = 192


route_scale = 2.827
norm_eps = 1e-06


def softmax_parts(score_cache, score_new):
    row_peak = jnp.maximum(jnp.max(score_cache, axis=-1), jnp.max(score_new, axis=-1))
    exp_cache = jnp.exp(score_cache - row_peak[..., None])
    exp_new = jnp.exp(score_new - row_peak[..., None])
    exp_total = jnp.sum(exp_cache, axis=-1) + jnp.sum(exp_new, axis=-1)
    prob_cache = (exp_cache / exp_total[..., None]).astype(jnp.bfloat16)
    prob_new = (exp_new / exp_total[..., None]).astype(jnp.bfloat16)
    return (prob_cache, prob_new)


def attention(cache_kv, new_kv, queries, lengths):
    score_scale = 1.0 / math.sqrt(QK)
    cache_len = cache_kv.shape[1]
    step_count = new_kv.shape[1]
    score_new = (
        jnp.einsum("bshk,btk->bsht", queries, new_kv, preferred_element_type=jnp.float32)
        * score_scale
    )
    step_ids = jnp.arange(step_count, dtype=jnp.int32)
    causal = step_ids[None, :] <= step_ids[:, None]
    score_new = jnp.where(causal[None, :, None, :], score_new, -jnp.inf)
    score_cache = (
        jnp.einsum("bshk,bpk->bshp", queries, cache_kv, preferred_element_type=jnp.float32)
        * score_scale
    )
    position = jnp.arange(cache_len, dtype=jnp.int32)
    is_live = position[None, :] < lengths[:, None]
    score_cache = jnp.where(is_live[:, None, None, :], score_cache, -jnp.inf)
    prob_cache, prob_new = softmax_parts(score_cache, score_new)
    context = jnp.einsum(
        "bshp,bpc->bshc", prob_cache, cache_kv[:, :, :LAT], preferred_element_type=jnp.float32
    )
    context = context + jnp.einsum(
        "bsht,btc->bshc", prob_new, new_kv[:, :, :LAT], preferred_element_type=jnp.float32
    )
    return context.astype(jnp.bfloat16)


def expert_ffn(token_rows, w_gate, w_up, w_down):
    gate = jnp.dot(token_rows, w_gate, preferred_element_type=jnp.float32)
    upward = jnp.dot(token_rows, w_up, preferred_element_type=jnp.float32)
    act = (jax.nn.silu(gate) * upward).astype(jnp.bfloat16)
    return jnp.dot(act, w_down, preferred_element_type=jnp.float32)


def route_weights(token_rows, route_ids, router):
    logits = jnp.dot(token_rows, router, preferred_element_type=jnp.float32)
    expert_range = jnp.arange(router.shape[1], dtype=jnp.int32)
    is_pick = route_ids[:, :, None] == expert_range[None, None, :]
    picked = jnp.sum(jnp.where(is_pick, logits[:, None, :], 0.0), axis=-1)
    gates = jax.nn.sigmoid(picked)
    return route_scale * gates / jnp.sum(gates, axis=1, keepdims=True)


def body(
    cache_kv,
    new_kv,
    queries,
    lengths,
    resid,
    value_up,
    out_proj,
    norm_gain,
    router,
    expert_ids,
    slots,
    w_gate,
    w_up,
    w_down,
):
    devices = lax.axis_size("ep")
    context = attention(cache_kv, new_kv, queries, lengths)
    tok_count = context.shape[0] * context.shape[1]
    context = context.reshape(tok_count, H, LAT)
    value_cols = value_up.shape[1]
    heads_per = max(1, value_cols // VH)
    outgoing = jnp.repeat(context, VH // value_cols, axis=1)
    arrived = lax.all_to_all(outgoing, "ep", split_axis=1, concat_axis=0, tiled=True)
    value_table = value_up.reshape(LAT, heads_per, value_cols // heads_per)
    values = jnp.einsum("rhc,chv->rhv", arrived, value_table, preferred_element_type=jnp.float32)
    values = values.astype(jnp.bfloat16).reshape(devices * tok_count, value_cols)
    turned = lax.all_to_all(out_proj, "ep", split_axis=1, concat_axis=0, tiled=True)
    column_share = jnp.dot(
        lax.all_gather(values, "ep", axis=1, tiled=True), turned, preferred_element_type=jnp.float32
    )
    attended = lax.all_to_all(column_share, "ep", split_axis=0, concat_axis=1, tiled=True)
    hidden = resid.reshape(tok_count, D).astype(jnp.float32) + attended
    mean_square = jnp.mean(hidden * hidden, axis=-1, keepdims=True)
    normed = (hidden * lax.rsqrt(mean_square + norm_eps) * norm_gain.astype(jnp.float32)).astype(
        jnp.bfloat16
    )
    route_ids = expert_ids.reshape(tok_count, TOP)
    route_slots = slots.reshape(tok_count, TOP)
    group_size = devices // EXPERTS
    weights = route_weights(normed, route_ids, router)
    expert_grid = (
        route_ids[:, :, None] == jnp.arange(EXPERTS, dtype=jnp.int32)[None, None, :]
    ).astype(jnp.float32)
    slot_grid = (route_slots[:, :, None] == jnp.arange(CAP, dtype=jnp.int32)[None, None, :]).astype(
        jnp.float32
    )
    places = jnp.sum(expert_grid[:, :, :, None] * slot_grid[:, :, None, :], axis=1)
    shares = jnp.sum(
        expert_grid[:, :, :, None] * slot_grid[:, :, None, :] * weights[:, :, None, None], axis=1
    )
    places_dest = jnp.repeat(places, group_size, axis=1)
    shares_dest = jnp.repeat(shares, group_size, axis=1)
    outgoing_rows = jnp.einsum(
        "tjc,td->jcd", places_dest.astype(jnp.bfloat16), normed, preferred_element_type=jnp.float32
    ).astype(jnp.bfloat16)
    slot_rows = lax.all_to_all(outgoing_rows, "ep", split_axis=0, concat_axis=0, tiled=True)
    flat_rows = slot_rows.reshape(-1, slot_rows.shape[2])
    produced = expert_ffn(flat_rows, w_gate, w_up, w_down)
    produced = produced.reshape(slot_rows.shape[0], slot_rows.shape[1], produced.shape[1])
    returned = lax.all_to_all(
        produced.astype(jnp.bfloat16), "ep", split_axis=0, concat_axis=0, tiled=True
    ).astype(produced.dtype)
    expert_mix = jnp.dot(
        shares_dest.reshape(tok_count, devices * CAP),
        returned.reshape(devices * CAP, D),
        precision=lax.Precision.HIGHEST,
    )
    mixed = (hidden + expert_mix).astype(jnp.bfloat16)
    return mixed.reshape(resid.shape)


def solution(mesh):
    return jax.shard_map(
        body,
        mesh=mesh,
        in_specs=(
            P(("rep", "ep"), None, None),
            P(("rep", "ep"), None, None),
            P(("rep", "ep"), None, None, None),
            P(("rep", "ep")),
            P(("rep", "ep"), None, None),
            P(None, "ep"),
            P("ep", None),
            P(),
            P(),
            P(("rep", "ep"), None, None),
            P(("rep", "ep"), None, None),
            P(None, "ep"),
            P(None, "ep"),
            P("ep", None),
        ),
        out_specs=P(("rep", "ep"), None, None),
        check_vma=False,
    )
```

profile of v0, /device:TPU:33, one launch (start us, length us, event | category | flops | bytes accessed | tf_op | source)
XLA Modules:
  0.0 690.7 jit_solution(3392303585385041434)
XLA Ops:
  7.5 3.8 fusion.41
  14.4 63.1 %all_to_all.60 = bf16[4,128,512]{2,0,1:T(4,128)(2,1)S(1)} all-to-all(bf16[4,128,512]{2,0,1:T(4,128)(2,1)S(1)} %bitcast.75), channel_id=1, replica_groups=mesh['rep'=2,'ep'=128] {'ep'}, dimensions={1} | all-to-all | bytes 1048576 | tf_op jit(solution)/shard_map/all_to_all | solution.py:99
  78.6 2.6 copy.54
  81.2 3.4 reshape.151
  84.7 71.3 %all_to_all.61 = bf16[128,2,1792]{2,1,0:T(2,128)(2,1)} all-to-all(bf16[128,2,1792]{2,1,0:T(2,128)(2,1)S(1)} %reshape.151), channel_id=1, replica_groups=mesh['rep'=2,'ep'=128] {'ep'}, dimensions={0} | all-to-all | bytes 1835008 | tf_op jit(solution)/shard_map/all_to_all | solution.py:103
  156.0 4.3 reshape.152
  161.9 1.8 copy.43
  163.7 3.1 reshape.147
  166.8 53.8 %all-gather.2.cloned.1.call-done = bf16[512,8192]{0,1:T(8,128)(2,1)} async-done(((bf16[512,64]{0,1:T(8,128)(2,1)}), bf16[512,8192]{0,1:T(8,128)(2,1)}) %all-gather.2.cloned.1.call-update) | async-done | bytes 8388624 | tf_op jit(solution)/shard_map/all_gather | solution.py:105
  220.6 11.4 %copy.41 = bf16[512,8192]{1,0:T(8,128)(2,1)} copy(bf16[512,8192]{0,1:T(8,128)(2,1)} %all-gather.2.cloned.1.call-done) | data formatting | bytes 16777216 | tf_op jit(solution)/shard_map/all_gather | solution.py:105
  232.0 13.1 %dot_general.43 = bf16[128,4,8192]{2,1,0:T(4,128)(2,1)} reshape(bf16[512,8192]{1,0:T(8,128)(2,1)} %copy.41) | data formatting | bytes 16777216 | tf_op jit(solution)/shard_map/dot_general | solution.py:104
  245.1 12.4 %fusion = f32[128,4,56]{0,2,1:T(8,128)S(1)} fusion(bf16[8192,56,1]{0,1,2:T(8,128)(2,1)S(1)} %reshape.147, bf16[128,4,8192]{2,1,0:T(4,128)(2,1)} %dot_general.43), kind=kOutput, calls=%fused_computation.2 | convolution fusion | flops 469762048 | bytes 9420800 | tf_op jit(solution)/shard_map/dot_general | solution.py:104
  258.6 11.5 %all-to-all-start.2 = ((f32[128,1,224]{2,1,0:T(1,128)}), f32[128,1,224]{2,1,0:T(1,128)S(1)}, u32[]{:S(2)}, u32[]{:S(2)}) async-start(f32[128,1,224]{2,1,0:T(1,128)} %reshape.153), calls=%async_computation.2 | async-start | bytes 262144 | tf_op jit(solution)/shard_map/all_to_all | solution.py:107
  270.6 16.2 %all-to-all-done.2 = f32[128,1,224]{2,1,0:T(1,128)S(1)} async-done(((f32[128,1,224]{2,1,0:T(1,128)}), f32[128,1,224]{2,1,0:T(1,128)S(1)}, u32[]{:S(2)}, u32[]{:S(2)}) %all-to-all-start.2) | async-done | bytes 114720 | tf_op jit(solution)/shard_map/all_to_all | solution.py:107
  291.4 3.8 copy.49
  295.2 172.5 %all_to_all.62 = bf16[128,2,7168]{2,1,0:T(2,128)(2,1)} all-to-all(bf16[128,2,7168]{2,1,0:T(2,128)(2,1)S(1)} %copy.49), channel_id=1, replica_groups=mesh['rep'=2,'ep'=128] {'ep'}, dimensions={0} | all-to-all | bytes 7340032 | tf_op jit(solution)/shard_map/all_to_all | solution.py:132
  467.7 8.4 %reshape.138 = bf16[256,7168]{1,0:T(8,128)(2,1)} reshape(bf16[128,2,7168]{2,1,0:T(2,128)(2,1)} %all_to_all.62) | data formatting | bytes 7340032 | tf_op jit(solution)/shard_map/reshape | solution.py:133
  476.1 3.7 fusion.43
  479.8 6.6 convolution_convert_fusion
  486.4 8.1 %convert_element_type.95 = bf16[128,2,7168]{2,1,0:T(2,128)(2,1)} reshape(bf16[256,7168]{1,0:T(8,128)(2,1)} %convolution_convert_fusion) | data formatting | bytes 7340032 | tf_op jit(solution)/shard_map/convert_element_type | solution.py:137
  494.5 13.3 %all-to-all-start.4 = ((bf16[128,2,7168]{2,1,0:T(2,128)(2,1)}), bf16[128,2,7168]{2,1,0:T(2,128)(2,1)}, u32[]{:S(2)}, u32[]{:S(2)}) async-start(bf16[128,2,7168]{2,1,0:T(2,128)(2,1)} %convert_element_type.95), calls=%async_computation.4 | async-start | bytes 7340032 | tf_op jit(solution)/shard_map/all_to_all | solution.py:136
  507.9 163.0 %all-to-all-done.4 = bf16[128,2,7168]{2,1,0:T(2,128)(2,1)} async-done(((bf16[128,2,7168]{2,1,0:T(2,128)(2,1)}), bf16[128,2,7168]{2,1,0:T(2,128)(2,1)}, u32[]{:S(2)}, u32[]{:S(2)}) %all-to-all-start.4) | async-done | bytes 3670048 | tf_op jit(solution)/shard_map/all_to_all | solution.py:136
  670.9 8.4 %reshape.139 = bf16[256,7168]{1,0:T(8,128)(2,1)} reshape(bf16[128,2,7168]{2,1,0:T(2,128)(2,1)} %all-to-all-done.4) | data formatting | bytes 7340032 | tf_op jit(solution)/shard_map/reshape | solution.py:141
  679.4 3.6 fusion.2
  (65 shorter events, 13.5 us)
Async XLA Ops:
  6.5 473.2 %copy-start = (bf16[128,7168]{1,0:T(8,128)(2,1)S(1)}, bf16[128,7168]{1,0:T(8,128)(2,1)}, u32[]{:S(2)}) copy-start(bf16[128,7168]{1,0:T(8,128)(2,1)} %param.27) | copy-start | bytes 5505028
  6.6 214.1 %all-gather.2.cloned.1.call-start = ((), (), s32[]{:S(2)}) async-start(), calls=%async_computation.5 | async-start | bytes 8454144 | tf_op jit(solution)/shard_map/all_gather | solution.py:105
  7.4 3.8 copy-start.2
  7.4 3.8 copy-start.8
  7.5 4.6 copy-start.1
  13.8 63.9 %copy-start.5 = (bf16[512,64]{0,1:T(8,128)(2,1)S(1)}, bf16[512,64]{0,1:T(8,128)(2,1)}, u32[]{:S(2)}) copy-start(bf16[512,64]{0,1:T(8,128)(2,1)} %param.19) | copy-start | bytes 196612
  245.1 25.1 %copy-start.4 = (bf16[2,2,7168]{2,1,0:T(2,128)(2,1)S(1)}, bf16[2,2,7168]{2,1,0:T(2,128)(2,1)}, u32[]{:S(2)}) copy-start(bf16[2,2,7168]{2,1,0:T(2,128)(2,1)} %param.18) | copy-start | bytes 172036
  245.1 25.3 %copy-start.6 = (bf16[7168]{0:T(1024)(128)(2,1)S(1)}, bf16[7168]{0:T(1024)(128)(2,1)}, u32[]{:S(2)}) copy-start(bf16[7168]{0:T(1024)(128)(2,1)} %param.21) | copy-start | bytes 43012
  245.1 25.5 %copy-start.9 = (s32[2,2,8]{2,1,0:T(2,128)S(1)}, s32[2,2,8]{2,1,0:T(2,128)}, u32[]{:S(2)}) copy-start(s32[2,2,8]{2,1,0:T(2,128)} %param.24) | copy-start | bytes 388
  245.1 25.5 %copy-start.7 = (s32[2,2,8]{2,1,0:T(2,128)S(1)}, s32[2,2,8]{2,1,0:T(2,128)}, u32[]{:S(2)}) copy-start(s32[2,2,8]{2,1,0:T(2,128)} %param.23) | copy-start | bytes 388
  257.5 31.5 %copy-start.3 = (bf16[7168,16]{0,1:T(8,128)(2,1)S(1)}, bf16[7168,16]{0,1:T(8,128)(2,1)}, u32[]{:S(2)}) copy-start(bf16[7168,16]{0,1:T(8,128)(2,1)} %param.22) | copy-start | bytes 688132
  258.6 28.3 %all-to-all-start.2 = ((f32[128,1,224]{2,1,0:T(1,128)}), f32[128,1,224]{2,1,0:T(1,128)S(1)}, u32[]{:S(2)}, u32[]{:S(2)}) async-start(f32[128,1,224]{2,1,0:T(1,128)} %reshape.153), calls=%async_computation.2 | async-start | bytes 262144 | tf_op jit(solution)/shard_map/all_to_all | solution.py:107
  494.5 176.4 %all-to-all-start.4 = ((bf16[128,2,7168]{2,1,0:T(2,128)(2,1)}), bf16[128,2,7168]{2,1,0:T(2,128)(2,1)}, u32[]{:S(2)}, u32[]{:S(2)}) async-start(bf16[128,2,7168]{2,1,0:T(2,128)(2,1)} %convert_element_type.95), calls=%async_computation.4 | async-start | bytes 7340032 | tf_op jit(solution)/shard_map/all_to_all | solution.py:136
Sparse Core Ops, SparseCore 0:
  78.7 141.8 all-gather.1
where the time goes:
time: 702 us; the launch traced here: 691 us
  blocking collectives  307 us (44%)
  waiting for transfers between devices  233 us (33%)
  local copies, waits for them, and re-layouts  74 us (11%)
  matrix products  34.7 us (5%)
  starting transfers between devices  24.8 us (4%)
  between operations  14 us (2%)
    all_to_all x1, blocking collectives, body(): lax.all_to_all(outgoing_rows, 'ep', split_axis=0, concat_axis=0, tiled=True)  172 us
    all_to_all x1, waiting for transfers between devices, body(): lax.all_to_all(produced.astype(jnp.bfloat16), 'ep', split_axis=0, concat_...  163 us
    all_to_all x1, blocking collectives, body(): lax.all_to_all(out_proj, 'ep', split_axis=1, concat_axis=0, tiled=True)  71.3 us
    all_to_all x1, blocking collectives, body(): lax.all_to_all(outgoing, 'ep', split_axis=1, concat_axis=0, tiled=True)  63.1 us
    all_gather x1, waiting for transfers between devices, body(): lax.all_gather(values, 'ep', axis=1, tiled=True)  53.8 us
    all_to_all x1, waiting for transfers between devices, body(): lax.all_to_all(column_share, 'ep', split_axis=0, concat_axis=1, tiled=True)  16.2 us
  transfers between devices with their start and end apart: 3, of which 3 were waited for; matrix products, arithmetic and copies ran while one was open for 3% of the time, Pallas kernels for 0%

commit v1 on v0

v1 whole, which is shorter than its diff:
```python
import functools
import math

import jax
import jax.numpy as jnp
from jax import lax
from jax.experimental import pallas as pl
from jax.experimental.pallas import tpu as pltpu
from jax.sharding import PartitionSpec as P

NX, NZ, NC = 4, 16, 2
DEV = NX * NC
HALF = NZ // 2

D = 7168
H = 64
LAT = 512
VH = 128
KV = 576
EXPERTS = 16
TOP = 8
CAP = 2
QK = 192
TOK = 4
UNITS = 128
ROW = DEV * TOK
SLOT = DEV * CAP
DX = D // NX
EXT = 128
DC = DX + EXT
JX = DX // 128
MSG = 64
LANE_SUM = 32
LANE_TAB = 64
QUAD = EXPERTS // NX
CHIPS_PER = NZ // QUAD

route_scale = 2.827
norm_eps = 1e-06

SUBS = ((0, 640), (640, 640), (1280, 512))
SUBS_AG = ((0, 640), (640, 640), (1280, 640))
NS = len(SUBS)

F32 = jnp.float32
BF16 = jnp.bfloat16


def mo(value, by):
    return pl.multiple_of(value, by)


def nt(a, b):
    return lax.dot_general(a, b, (((1,), (1,)), ((), ())), preferred_element_type=F32)


def nn(a, b):
    return lax.dot_general(a, b, (((1,), (0,)), ((), ())), preferred_element_type=F32)


def iota(shape, axis):
    return lax.broadcasted_iota(jnp.int32, shape, axis)


def kernel(
    cache_h, new_ref, q_h, len_ref, resid_ref, vu_h, wo_h, gain_ref, router_h, ids_ref, slots_ref, wg_h, wu_h, wd_h,
    out_ref,
    cache_v, q_v, score_v, stage_v, ctx_v, arr_v, arrf_v, vu_v, val_v, wo_v, rs_in, rs_out, hid_v, tab_s, tab_v,
    ress_v, resf_v, res_v, resw_v, rout_v, ag_v, dsp_v, d_v, wgu_v, act_s, act_v, wd_v, rs2_in, rs2_out, fin_v, fin_s, at_v,
    l_cache, l_misc, l_weights,
    s_ctx, s_small, s_w, s_wd, s_val, s_rs, s_ag, s_dsp, s_act, s_rs2, s_out,
    r_ctx, r_small, r_wo, r_vu, r_gu, r_wd, r_val, r_rs, r_ag, r_dsp, r_act, r_rs2, r_out,
    go_sem,
):
    me = lax.axis_index("ep")
    c = lax.rem(me, NC)
    z = lax.rem(me // NC, NZ)
    x = me // (NC * NZ)
    dev = x * NC + c
    quad = z // CHIPS_PER

    def idx(xx, zz, cc):
        return {"ep": (xx * NZ + zz) * NC + cc}

    def wrap(zz):
        return lax.rem(zz + 2 * NZ, NZ)

    def xwrap(xx):
        return lax.rem(xx, NX)

    def send(src, dst, ssem, rsem, to):
        pltpu.make_async_remote_copy(src_ref=src, dst_ref=dst, send_sem=ssem, recv_sem=rsem, device_id=to).start()

    def arrived(ref, sem):
        pltpu.make_async_copy(ref, ref, sem).wait()

    main = c == 1
    side = c == 0

    bar = pltpu.get_barrier_semaphore()

    @pl.when(main)
    def _():
        def greet(i, carry):
            @pl.when(i != me)
            def _():
                pl.semaphore_signal(bar, inc=1, device_id={"ep": i})
            return carry
        lax.fori_loop(0, NX * NZ * NC, greet, 0)

    @pl.when(side)
    def _():
        for xx in range(NX):
            pl.semaphore_signal(bar, inc=1, device_id=idx(xx, z, 1))

    loads = [pltpu.make_async_copy(q_h, q_v, l_misc)]
    loads += [pltpu.make_async_copy(cache_h.at[b], cache_v.at[b], l_cache.at[b]) for b in range(2)]
    for load in loads:
        load.start()

    rows8, lanes8 = iota((8, 128), 0), iota((8, 128), 1)
    table = jnp.zeros((8, 128), F32)
    for t in range(TOK):
        for k in range(TOP):
            hit = (rows8 == t) & (lanes8 == ids_ref[t // 2, t % 2, k] + LANE_TAB)
            table = jnp.where(hit, (slots_ref[t // 2, t % 2, k] + 1).astype(F32), table)
    tab_s[...] = table

    resf_v[...] = jnp.zeros_like(resf_v)
    for t in range(TOK):
        row = resid_ref[t // 2, pl.ds(t % 2, 1), :].astype(F32)
        for xx in range(NX):
            for j in range(JX):
                col = xx * DX + j * 128
                resf_v[pl.ds(xx * MSG + t * JX + j, 1), :] = row[:, col:col + 128]
    ress_v[...] = resf_v[pl.ds(0, NX * MSG), :].reshape(NX, MSG, 128).astype(BF16)

    scale = 1.0 / math.sqrt(QK)
    blk = 512
    nblk = cache_v.shape[2] // blk
    loads[0].wait()
    for b in range(2):
        qb = q_v[b]
        qf = qb.astype(F32)
        step_of = iota((2 * H, 1), 0) // H
        new_rows = [new_ref[b, pl.ds(t, 1), :].astype(F32) for t in range(2)]
        s_new = [jnp.sum(qf * row, axis=1, keepdims=True) * scale for row in new_rows]
        s_new[1] = jnp.where(step_of >= 1, s_new[1], -jnp.inf)
        peak = jnp.maximum(s_new[0], s_new[1])
        loads[1 + b].wait()
        for p in range(nblk):
            sc = nn(qb, cache_v[b, :, pl.ds(p * blk, blk)]) * scale
            pos = iota((2 * H, blk), 1) + p * blk
            sc = jnp.where(pos < len_ref[b], sc, -jnp.inf)
            score_v[:, pl.ds(p * blk, blk)] = sc
            peak = jnp.maximum(peak, jnp.max(sc, axis=1, keepdims=True))
        p_new = [jnp.exp(s - peak) for s in s_new]
        total = p_new[0] + p_new[1]
        acc = p_new[0].astype(BF16).astype(F32) * new_rows[0][:, :LAT]
        acc = acc + p_new[1].astype(BF16).astype(F32) * new_rows[1][:, :LAT]
        for p in range(nblk):
            pr = jnp.exp(score_v[:, pl.ds(p * blk, blk)] - peak)
            total = total + jnp.sum(pr, axis=1, keepdims=True)
            acc = acc + nt(pr.astype(BF16), cache_v[b, pl.ds(0, LAT), pl.ds(p * blk, blk)])
        ctx = acc / total
        for s in range(2):
            for j in range(LAT // 128):
                stage_v[pl.ds(j * TOK + b * 2 + s, H, stride=16), :] = ctx[s * H:(s + 1) * H, j * 128:(j + 1) * 128]
    ctx_v[...] = stage_v[...].reshape(H, 16, 128).astype(BF16)

    @pl.when(main)
    def _():
        pl.semaphore_wait(bar, NX * NZ - 1 + NX)

    @pl.when(side)
    def _():
        pl.semaphore_wait(bar, NX * NZ)

    def ctx_send(o, carry):
        far = HALF - (o + 1) // 2
        zz = wrap(jnp.where(lax.rem(o, 2) == 1, z + far, z - far))
        for i in range(NX):
            xx = xwrap(x + i + 1)
            own = main & (zz == z) & (xx == x)

            @pl.when(jnp.logical_not(own))
            def _():
                send(ctx_v.at[xx * NZ + zz], arr_v.at[z, dev], s_ctx, r_ctx.at[z], idx(xx, zz, 1))

            @pl.when(own)
            def _():
                arr_v[z, dev] = ctx_v[xx * NZ + zz]
        return carry
    lax.fori_loop(0, NZ, ctx_send, 0)

    wo_row = mo(x * VH + c * (VH // NC), VH // NC)
    for xx in range(NX):
        other = jnp.logical_not(main & (x == xx))
        columns = pl.ds(xx * DX, DX)

        @pl.when(other)
        def _():
            send(tab_s, tab_v.at[dev], s_small.at[0], r_small.at[0], idx(xx, z, 1))
            send(ress_v.at[xx], res_v.at[dev], s_small.at[1], r_small.at[1], idx(xx, z, 1))
            send(wo_h.at[:, columns], wo_v.at[pl.ds(wo_row, VH // NC), :], s_w.at[0], r_wo, idx(xx, z, 1))

        @pl.when(jnp.logical_not(other))
        def _():
            tab_v[dev] = tab_s[...]
            res_v[dev] = ress_v[xx]
            pltpu.make_async_copy(wo_h.at[:, columns], wo_v.at[pl.ds(wo_row, VH // NC), :], l_weights.at[0]).start()

    gate_at = pl.ds(mo(c * UNITS, UNITS), UNITS)
    up_at = pl.ds(mo((NC + c) * UNITS, UNITS), UNITS)
    wd_row = mo((x * NC + c) * UNITS, UNITS)

    def wd_send():
        for xx in range(NX):
            columns = pl.ds(xx * DX, DX)
            other = jnp.logical_not(main & (x == xx))

            @pl.when(other)
            def _():
                send(wd_h.at[:, columns], wd_v.at[pl.ds(wd_row, UNITS), :], s_wd, r_wd, idx(xx, z, 1))

            @pl.when(jnp.logical_not(other))
            def _():
                pltpu.make_async_copy(wd_h.at[:, columns], wd_v.at[pl.ds(wd_row, UNITS), :], l_weights.at[3]).start()

    def pick_lanes():
        jj, lane = iota((NX * SLOT, 128), 0), iota((NX * SLOT, 128), 1)
        return jnp.where(lane == LANE_TAB + (jj // SLOT) * QUAD + quad, 1.0, 0.0).astype(BF16)

    @pl.when(main)
    def _main():
        vu_copy = pltpu.make_async_copy(vu_h, vu_v.at[pl.ds(VH // NC, VH // NC), :], l_misc)
        vu_copy.start()
        send(wg_h, wgu_v.at[:, gate_at], s_w.at[1], r_gu, idx(x, z, 0))
        send(wu_h, wgu_v.at[:, up_at], s_w.at[2], r_gu, idx(x, z, 0))
        rout_v[...] = jnp.zeros_like(rout_v)
        rout_copy = pltpu.make_async_copy(
            router_h.at[:, pl.ds(mo(x * DX, 128), DX)], rout_v.at[pl.ds(0, EXPERTS), :], l_weights.at[1]
        )
        rout_copy.start()
        vu_copy.wait()
        arrived(vu_v.at[pl.ds(0, VH // NC), :], r_vu)

        own_lanes = pl.ds(mo(x * VH, VH), VH)

        def ctx_row(r):
            @pl.when(r == z)
            def _():
                arrived(arr_v.at[r, pl.ds(0, DEV - 1)], r_ctx.at[r])

            @pl.when(r != z)
            def _():
                arrived(arr_v.at[r], r_ctx.at[r])

            arrf_v[...] = arr_v[r].reshape(DEV * 16, 128).astype(F32)
            cols = []
            for j in range(LAT // 128):
                cols.append(jnp.concatenate(
                    [arrf_v[pl.ds(j * TOK + t, DEV, stride=16), :] for t in range(TOK)], axis=0))
            rows = jnp.concatenate(cols, axis=1).astype(BF16)
            val_v[r, :, own_lanes] = nt(rows, vu_v[...]).astype(BF16)
            for i in range(NX - 1):
                send(val_v.at[r, :, own_lanes], val_v.at[r, :, own_lanes], s_val, r_val.at[r],
                     idx(xwrap(x + i + 1), z, 1))

        def val_wait(r):
            arrived(val_v.at[r, :, pl.ds(0, (NX - 1) * VH)], r_val.at[r])

        def chain(rows2, weights, in_ref, out_buf, ssem, rsem, s):
            up, down = idx(x, wrap(z + 1), 1), idx(x, wrap(z - 1), 1)
            for i, (o, w) in enumerate(SUBS):
                part = nn(rows2, weights[:, o:o + w])

                @pl.when(s >= 1)
                def _():
                    arrived(in_ref.at[0, s, :, pl.ds(o, w)], rsem.at[0, s, i])
                first = part[:ROW] + in_ref[0, s, :, pl.ds(o, w)].astype(F32)
                out_buf[0, s, :, pl.ds(o, w)] = first.astype(BF16)
                send(out_buf.at[0, s, :, pl.ds(o, w)], in_ref.at[0, s + 1, :, pl.ds(o, w)], ssem.at[0],
                     rsem.at[0, s + 1, i], up)

                @pl.when(s >= 2)
                def _():
                    arrived(in_ref.at[1, s, :, pl.ds(o, w)], rsem.at[1, s, i])

                @pl.when(s >= 1)
                def _():
                    second = part[ROW:] + in_ref[1, s, :, pl.ds(o, w)].astype(F32)
                    out_buf[1, s, :, pl.ds(o, w)] = second.astype(BF16)
                    send(out_buf.at[1, s, :, pl.ds(o, w)], in_ref.at[1, s + 1, :, pl.ds(o, w)], ssem.at[1],
                         rsem.at[1, s + 1, i], down)

        def chain_end(in_ref, rsem, o, w, i):
            for d in range(2):
                arrived(in_ref.at[d, HALF, :, pl.ds(o, w)], rsem.at[d, HALF, i])
            return in_ref[0, HALF, :, pl.ds(o, w)].astype(F32) + in_ref[1, HALF, :, pl.ds(o, w)].astype(F32)

        def chain_zero(in_ref):
            in_ref[0, 0] = jnp.zeros((ROW, DX), BF16)
            in_ref[1, 1] = jnp.zeros((ROW, DX), BF16)

        chain_zero(rs_in)
        chain_zero(rs2_in)

        ctx_row(wrap(z + HALF))
        ctx_row(wrap(z + HALF - 1))
        ctx_row(wrap(z - HALF + 1))
        pltpu.make_async_copy(
            wo_h.at[:, pl.ds(0, DX)], wo_v.at[pl.ds(wo_row, VH // NC), :], l_weights.at[0]).wait()
        arrived(wo_v.at[pl.ds(0, (DEV - 1) * (VH // NC)), :], r_wo)

        def rs_step(s, carry):
            ahead = HALF - 2 - s

            @pl.when(ahead >= 0)
            def _():
                ctx_row(wrap(z + ahead))

            @pl.when(ahead >= 1)
            def _():
                ctx_row(wrap(z - ahead))

            @pl.when(ahead == 0)
            def _():
                pl.semaphore_signal(go_sem, inc=1, device_id=idx(x, z, 0))
                wd_send()
            ra, rb = wrap(z + HALF - s), wrap(z - HALF + s)
            val_wait(ra)

            @pl.when(s >= 1)
            def _():
                val_wait(rb)
            rows2 = jnp.concatenate([val_v[ra], val_v[rb]], axis=0)
            chain(rows2, wo_v, rs_in, rs_out, s_rs, r_rs, s)
            return carry
        lax.fori_loop(0, HALF, rs_step, 0)

        val_wait(z)
        arrived(res_v.at[pl.ds(0, DEV - 1)], r_small.at[1])
        arrived(tab_v.at[pl.ds(0, DEV - 1)], r_small.at[0])
        resw_v[...] = res_v[...].reshape(DEV * MSG, 128).astype(F32)
        own_rows = val_v[z]
        sums = jnp.zeros((ROW, 1), F32)
        for i, (o, w) in enumerate(SUBS):
            part = nn(own_rows, wo_v[:, o:o + w]) + chain_end(rs_in, r_rs, o, w, i)
            res = []
            for j in range(o // 128, (o + w) // 128):
                res.append(jnp.concatenate(
                    [resw_v[pl.ds(t * JX + j, DEV, stride=MSG), :] for t in range(TOK)], axis=0))
            hidden = part + jnp.concatenate(res, axis=1)
            hid_v[:, pl.ds(o, w)] = hidden
            sums = sums + jnp.sum(hidden * hidden, axis=1, keepdims=True)
            gain = gain_ref[:, pl.ds(mo(x * DX + o, 128), w)].astype(F32)
            ag_v[z, :, pl.ds(o, w)] = (hidden * gain).astype(BF16)
        rout_copy.wait()
        logits = nt(ag_v[z, :, pl.ds(0, DX)], rout_v[...])
        lane = iota((ROW, 128), 1)
        high = logits.astype(BF16).astype(F32)
        sums_high = sums.astype(BF16).astype(F32)
        ext = high + pltpu.roll(logits - high, EXPERTS, 1)
        ext = jnp.where(lane == LANE_SUM, sums_high, ext)
        ext = jnp.where(lane == LANE_SUM + 1, sums - sums_high, ext)
        rows = iota((DEV, 128), 0)
        tabs = []
        for t in range(TOK):
            piece = jnp.zeros((DEV, 128), F32)
            for d in range(DEV):
                piece = jnp.where(rows == d, tab_v[d, pl.ds(t, 1), :], piece)
            tabs.append(piece)
        ext = ext + jnp.concatenate(tabs, axis=0)
        ag_v[z, :, pl.ds(DX, EXT)] = ext.astype(BF16)

        up, down = idx(x, wrap(z + 1), 1), idx(x, wrap(z - 1), 1)

        def ag_send(r, i, way):
            o, w = SUBS_AG[i]
            view = ag_v.at[r, :, pl.ds(o, w)]
            send(view, view, s_ag.at[way], r_ag.at[r, i], (up, down)[way])

        def ag_wait(r, i):
            o, w = SUBS_AG[i]
            arrived(ag_v.at[r, :, pl.ds(o, w)], r_ag.at[r, i])

        def dispatch(r):
            picked = nt(pick_lanes(), ag_v[r, :, pl.ds(DX, EXT)])
            jj, tok = iota((NX * SLOT, ROW), 0), iota((NX * SLOT, ROW), 1)
            wanted = (lax.rem(jj, SLOT) // DEV + 1).astype(F32)
            hit = (picked == wanted) & (lax.rem(jj, DEV) == lax.rem(tok, DEV))
            place = jnp.where(hit, 1.0, 0.0).astype(BF16)
            moved = nn(place, ag_v[r]).astype(BF16)
            dsp_v[r] = moved.reshape(NX, SLOT, DC)
            for i in range(NX):
                xx = xwrap(x + i + 1)
                send(dsp_v.at[r, xx], d_v.at[r, x], s_dsp, r_dsp.at[r], idx(xx, z, 0))

        for i in range(NS):
            ag_send(z, i, 0)
            ag_send(z, i, 1)
        dispatch(z)

        def ag_step(k, carry):
            ra, rb = wrap(z - k), wrap(z + k)
            for i in range(NS):
                ag_wait(ra, i)

                @pl.when(k < HALF)
                def _():
                    ag_send(ra, i, 0)
                    ag_wait(rb, i)

                @pl.when(k < HALF - 1)
                def _():
                    ag_send(rb, i, 1)
            dispatch(ra)

            @pl.when(k < HALF)
            def _():
                dispatch(rb)
            return carry
        lax.fori_loop(1, HALF + 1, ag_step, 0)

        pltpu.make_async_copy(
            wd_h.at[:, pl.ds(0, DX)], wd_v.at[pl.ds(wd_row, UNITS), :], l_weights.at[3]).wait()
        arrived(wd_v.at[pl.ds(0, (DEV - 1) * UNITS), :], r_wd)

        def act_rows(r):
            arrived(act_v.at[r], r_act.at[r])
            picked = nt(ag_v[r, :, pl.ds(DX, EXT)], pick_lanes())
            jj, tok = iota((ROW, NX * SLOT), 1), iota((ROW, NX * SLOT), 0)
            wanted = (lax.rem(jj, SLOT) // DEV + 1).astype(F32)
            hit = (picked == wanted) & (lax.rem(jj, DEV) == lax.rem(tok, DEV))
            place = jnp.where(hit, 1.0, 0.0).astype(BF16)
            return jnp.concatenate(
                [nn(place[:, i * SLOT:(i + 1) * SLOT], act_v[r, i]).astype(BF16) for i in range(NX)], axis=1)

        def rs2_step(s, carry):
            ra, rb = wrap(z + HALF - s), wrap(z - HALF + s)
            at_v[pl.ds(0, ROW), :] = act_rows(ra)

            @pl.when(s >= 1)
            def _():
                at_v[pl.ds(ROW, ROW), :] = act_rows(rb)
            chain(at_v[...], wd_v, rs2_in, rs2_out, s_rs2, r_rs2, s)
            return carry
        at_v[...] = jnp.zeros_like(at_v)
        lax.fori_loop(0, HALF, rs2_step, 0)

        rows_own = act_rows(z)
        for i, (o, w) in enumerate(SUBS):
            mixed = nn(rows_own, wd_v[:, o:o + w]) + chain_end(rs2_in, r_rs2, o, w, i) + hid_v[:, pl.ds(o, w)]
            for t in range(TOK):
                for j in range(o // 128, (o + w) // 128):
                    fin_v[pl.ds(t * JX + j, DEV, stride=MSG), :] = (
                        mixed[t * DEV:(t + 1) * DEV, j * 128 - o:j * 128 - o + 128])
        for t in range(TOK * JX, MSG):
            fin_v[pl.ds(t, DEV, stride=MSG), :] = jnp.zeros((DEV, 128), F32)
        fin_s[...] = fin_v[...].reshape(DEV, MSG, 128).astype(BF16)
        for i in range(DEV):
            to = lax.rem(dev + i + 1, DEV)

            if i < DEV - 1:
                send(fin_s.at[to], out_ref.at[x], s_out, r_out, idx(to // NC, z, lax.rem(to, NC)))
        out_ref[x] = fin_s[dev]
        arrived(out_ref.at[pl.ds(0, NX - 1)], r_out)

        arrived(ctx_v.at[pl.ds(0, NX * NZ - 1)], s_ctx)
        arrived(tab_v.at[pl.ds(0, NX - 1)], s_small.at[0])
        arrived(res_v.at[pl.ds(0, NX - 1)], s_small.at[1])
        arrived(wo_v.at[pl.ds(0, (NX - 1) * (VH // NC)), :], s_w.at[0])
        arrived(wgu_v.at[:, pl.ds(0, UNITS)], s_w.at[1])
        arrived(wgu_v.at[:, pl.ds(0, UNITS)], s_w.at[2])
        arrived(wd_v.at[pl.ds(0, (NX - 1) * UNITS), :], s_wd)
        arrived(val_v.at[:, :, pl.ds(0, (NX - 1) * VH)], s_val)
        for buf, sem in ((rs_out, s_rs), (rs2_out, s_rs2)):
            arrived(buf.at[0], sem.at[0])
            arrived(buf.at[1, pl.ds(1, HALF - 1)], sem.at[1])
        arrived(ag_v.at[pl.ds(0, HALF)], s_ag.at[0])
        arrived(ag_v.at[pl.ds(0, HALF - 1)], s_ag.at[1])
        arrived(dsp_v, s_dsp)
        arrived(fin_s.at[pl.ds(0, DEV - 1)], s_out)

    @pl.when(side)
    def _side():
        send(vu_h, vu_v.at[pl.ds(0, VH // NC), :], s_small.at[2], r_vu, idx(x, z, 1))
        own = [
            pltpu.make_async_copy(wg_h, wgu_v.at[:, gate_at], l_weights.at[1]),
            pltpu.make_async_copy(wu_h, wgu_v.at[:, up_at], l_weights.at[2]),
        ]
        for copy in own:
            copy.start()
        pl.semaphore_wait(go_sem, 1)
        wd_send()
        for copy in own:
            copy.wait()
        arrived(wgu_v.at[:, pl.ds(0, NC * UNITS)], r_gu)

        own_expert = x * QUAD + quad

        def experts(rows):
            for r in rows:
                arrived(d_v.at[r], r_dsp.at[r])
            both = jnp.zeros((SLOT * len(rows), 2 * NC * UNITS), F32)
            ext = jnp.zeros((SLOT * len(rows), EXT), F32)
            for xx in range(NX):
                both = both + nn(
                    jnp.concatenate([d_v[r, xx, :, pl.ds(0, DX)] for r in rows], axis=0),
                    wgu_v[xx * DX:(xx + 1) * DX, :])
                piece = jnp.concatenate([d_v[r, xx, :, pl.ds(DX, EXT)] for r in rows], axis=0).astype(F32)
                ext = ext + piece
            lane = iota(ext.shape, 1)
            squares = jnp.sum(
                jnp.where((lane == LANE_SUM) | (lane == LANE_SUM + 1), ext, 0.0), axis=1, keepdims=True)
            inv = lax.rsqrt(squares / D + norm_eps)
            logits = (ext + pltpu.roll(ext, EXT - EXPERTS, 1)) * inv
            named = (pltpu.roll(piece, EXT - LANE_TAB, 1) > 0.0) & (lane < EXPERTS)
            gates = jnp.where(named, 1.0 / (1.0 + jnp.exp(-logits)), 0.0)
            norm = jnp.sum(gates, axis=1, keepdims=True)
            mine = jnp.sum(jnp.where(lane == own_expert, gates, 0.0), axis=1, keepdims=True)
            share = jnp.where(norm > 0.0, route_scale * mine / norm, 0.0)
            gate = both[:, :NC * UNITS] * inv
            upward = both[:, NC * UNITS:] * inv
            act = (gate / (1.0 + jnp.exp(-gate)) * upward * share).astype(BF16)
            for i, r in enumerate(rows):
                act_s[r] = act[i * SLOT:(i + 1) * SLOT]
                for n in range(NX):
                    send(act_s.at[r], act_v.at[r, x], s_act, r_act.at[r], idx(xwrap(x + n), z, 1))

        experts([z])

        def step(k, carry):
            experts([wrap(z - k), wrap(z + k)])
            return carry
        lax.fori_loop(1, HALF, step, 0)
        experts([wrap(z + HALF)])

        arrived(out_ref, r_out)
        arrived(ctx_v, s_ctx)
        arrived(tab_v.at[pl.ds(0, NX)], s_small.at[0])
        arrived(res_v.at[pl.ds(0, NX)], s_small.at[1])
        arrived(vu_v.at[pl.ds(0, VH // NC), :], s_small.at[2])
        arrived(wo_v.at[pl.ds(0, NX * (VH // NC)), :], s_w.at[0])
        arrived(wd_v.at[pl.ds(0, NX * UNITS), :], s_wd)
        arrived(act_v, s_act)


def body(
    cache_kv, new_kv, queries, lengths, resid, value_up, out_proj, norm_gain, router, expert_ids, slots, w_gate, w_up,
    w_down,
):
    seqs, steps = resid.shape[:2]
    cache_len = cache_kv.shape[1]
    hbm = pl.BlockSpec(memory_space=pltpu.HBM)
    vmem = pl.BlockSpec(memory_space=pltpu.VMEM)
    smem = pl.BlockSpec(memory_space=pltpu.SMEM)
    dma = pltpu.SemaphoreType.DMA
    scratch = [
        pltpu.VMEM((seqs, KV, cache_len), BF16),
        pltpu.VMEM((seqs, steps * H, KV), BF16),
        pltpu.VMEM((steps * H, cache_len), F32),
        pltpu.VMEM((H * 16, 128), F32),
        pltpu.VMEM((H, 16, 128), BF16),
        pltpu.VMEM((NZ, DEV, 16, 128), BF16),
        pltpu.VMEM((DEV * 16, 128), F32),
        pltpu.VMEM((VH, LAT), BF16),
        pltpu.VMEM((NZ, ROW, NX * VH), BF16),
        pltpu.VMEM((NX * VH, DX), BF16),
        pltpu.VMEM((2, HALF + 1, ROW, DX), BF16),
        pltpu.VMEM((2, HALF, ROW, DX), BF16),
        pltpu.VMEM((ROW, DX), F32),
        pltpu.VMEM((8, 128), F32),
        pltpu.VMEM((DEV, 8, 128), F32),
        pltpu.VMEM((NX, MSG, 128), BF16),
        pltpu.VMEM((NX * MSG, 128), F32),
        pltpu.VMEM((DEV, MSG, 128), BF16),
        pltpu.VMEM((DEV * MSG, 128), F32),
        pltpu.VMEM((128, DX), BF16),
        pltpu.VMEM((NZ, ROW, DC), BF16),
        pltpu.VMEM((NZ, NX, SLOT, DC), BF16),
        pltpu.VMEM((NZ, NX, SLOT, DC), BF16),
        pltpu.VMEM((D, 2 * NC * UNITS), BF16),
        pltpu.VMEM((NZ, SLOT, NC * UNITS), BF16),
        pltpu.VMEM((NZ, NX, SLOT, NC * UNITS), BF16),
        pltpu.VMEM((NX * NC * UNITS, DX), BF16),
        pltpu.VMEM((2, HALF + 1, ROW, DX), BF16),
        pltpu.VMEM((2, HALF, ROW, DX), BF16),
        pltpu.VMEM((DEV * MSG, 128), F32),
        pltpu.VMEM((DEV, MSG, 128), BF16),
        pltpu.VMEM((2 * ROW, NX * NC * UNITS), BF16),
        dma((seqs,)), dma, dma((4,)),
        dma, dma((3,)), dma((3,)), dma, dma, dma((2,)), dma((2,)), dma, dma, dma((2,)), dma,
        dma((NZ,)), dma((2,)), dma, dma, dma, dma, dma((NZ,)), dma((2, HALF + 1, NS)), dma((NZ, NS)), dma((NZ,)),
        dma((NZ,)), dma((2, HALF + 1, NS)), dma,
        pltpu.SemaphoreType.REGULAR,
    ]
    out = pl.pallas_call(
        kernel,
        out_shape=jax.ShapeDtypeStruct((NX, MSG, 128), BF16),
        in_specs=[hbm, vmem, hbm, smem, vmem, hbm, hbm, vmem, hbm, smem, smem, hbm, hbm, hbm],
        out_specs=vmem,
        scratch_shapes=scratch,
        compiler_params=pltpu.CompilerParams(
            collective_id=0, has_side_effects=True, vmem_limit_bytes=(64 << 20) - (64 << 10)),
        name="layer",
    )(
        jnp.transpose(cache_kv, (0, 2, 1)), new_kv, queries.reshape(seqs, steps * H, KV), lengths, resid,
        value_up.T, out_proj, norm_gain.reshape(1, D), router.T, expert_ids, slots, w_gate, w_up, w_down,
    )
    out = out[:, :TOK * JX].reshape(NX, TOK, JX, 128).transpose(1, 0, 2, 3)
    return out.reshape(resid.shape)


def solution(mesh):
    return jax.shard_map(
        body,
        mesh=mesh,
        in_specs=(
            P(("rep", "ep"), None, None),
            P(("rep", "ep"), None, None),
            P(("rep", "ep"), None, None, None),
            P(("rep", "ep")),
            P(("rep", "ep"), None, None),
            P(None, "ep"),
            P("ep", None),
            P(),
            P(),
            P(("rep", "ep"), None, None),
            P(("rep", "ep"), None, None),
            P(None, "ep"),
            P(None, "ep"),
            P("ep", None),
        ),
        out_specs=P(("rep", "ep"), None, None),
        check_vma=False,
    )
```

time: 702 us -> 146 us (0.21); the launches traced: 691 us -> 146 us
  blocking collectives: 307 us -> 0 us
  waiting for transfers between devices: 233 us -> 0 us
  Pallas kernels: 0 us -> 143 us
  local copies, waits for them, and re-layouts: 74 us -> 2.85 us
  matrix products: 34.7 us -> 0 us
  starting transfers between devices: 24.8 us -> 0 us
  between operations: 14 us -> 0.02 us
    all_to_all x3 -> x0, blocking collectives: 307 us -> none  [the longest x1 172 us: body(): lax.all_to_all(outgoing_rows, 'ep', split_axis=0, concat_axis=0, tiled=True)]
    all_to_all x2 -> x0, waiting for transfers between devices: 179 us -> none  [the longest x1 163 us: body(): lax.all_to_all(produced.astype(jnp.bfloat16), 'ep', split_axis=0, concat_...]
    pallas_call x0 -> x1, Pallas kernels: none -> 143 us  [body(): pl.pallas_call(kernel, out_shape=jax.ShapeDtypeStruct((NX, MSG, 128), BF1...]
    all_gather x1 -> x0, waiting for transfers between devices: 53.8 us -> none  [body(): lax.all_gather(values, 'ep', axis=1, tiled=True)]
    dot_general x11 -> x0, matrix products: 34.7 us -> none  [the longest x1 12.4 us: body(): jnp.dot(lax.all_gather(values, 'ep', axis=1, tiled=True), turned, preferr...]
    all_to_all x2 -> x0, starting transfers between devices: 24.8 us -> none  [the longest x1 13.3 us: body(): lax.all_to_all(produced.astype(jnp.bfloat16), 'ep', split_axis=0, concat_...]
    reshape x4 -> x2, local copies, waits for them, and re-layouts: 17.7 us -> 1.99 us  [the longest x1 1.34 us: body(): norm_gain.reshape(1, D)]
    dot_general x2 -> x0, local copies, waits for them, and re-layouts: 13.2 us -> none  [body(): jnp.dot(lax.all_gather(values, 'ep', axis=1, tiled=True), turned, preferr...]
  transfers between devices with their start and end apart: 3 -> 0, of which waited for: 3 -> 0; matrix products, arithmetic and copies ran while one was open for 3% -> 0% of each run, Pallas kernels for 0% -> 0%
where the time goes in v1:
time: 146 us
  Pallas kernels  143 us (98%)
  local copies, waits for them, and re-layouts  2.85 us (2%)
    pallas_call x1, Pallas kernels, body(): pl.pallas_call(kernel, out_shape=jax.ShapeDtypeStruct((NX, MSG, 128), BF1...  143 us

profile of v1, /device:TPU:33, one launch (start us, length us, event | category | flops | bytes accessed | tf_op | source)
XLA Modules:
  0.0 145.7 jit_solution(5416885413885634559)
XLA Ops:
  0.0 1.3 reshape.13.gain_ref
  1.3 142.9 %layer.1 = bf16[4,64,128]{2,1,0:T(8,128)(2,1)} custom-call(bf16[2,576,2048]{2,1,0:T(8,128)(2,1)} %bitcast.7, bf16[2,2,576]{2,1,0:T(2,128)(2,1)} %new_ref.1, bf16[2,128,576]{2,1,0:T(8,128)(2,1)} %bitcast.8, s32[2]{0:T(128)} %len_ref.1, bf16[2,2,7168]{2,1,0:T(2,128)(2,1)} %resid_ref.1, bf16[64,512]{1,0:T(8,128)(2,1)} %bitcast.11, bf16[64,7168]{1,0:T(8,128)(2,1)} %wo_h.1, ...), custom_call_target="tpu_custom_call" | custom-call | tf_op jit(solution)/shard_map/layer/pallas_call | solution.py:599
  144.2 0.8 slice.3
  145.1 0.7 reshape.15
  (2 shorter events, 0.0 us)

commit v2 on v1

v2 whole, which is shorter than its diff:
```python
import functools
import math

import jax
import jax.numpy as jnp
from jax import lax
from jax.experimental import pallas as pl
from jax.experimental.pallas import tpu as pltpu
from jax.sharding import PartitionSpec as P

NX, NZ, NC = 4, 16, 2
DEV = NX * NC
HALF = NZ // 2

D = 7168
H = 64
LAT = 512
VH = 128
KV = 576
EXPERTS = 16
TOP = 8
CAP = 2
QK = 192
TOK = 4
UNITS = 128
ROW = DEV * TOK
SLOT = DEV * CAP
DX = D // NX
EXT = 128
DC = DX + EXT
JX = DX // 128
MSG = 64
LANE_SUM = 32
LANE_TAB = 64
QUAD = EXPERTS // NX
CHIPS_PER = NZ // QUAD

route_scale = 2.827
norm_eps = 1e-06

CUBE = 4

SUBS = tuple((256 * i, 256) for i in range(DX // 256))
SUBS_AG = SUBS[:-1] + ((SUBS[-1][0], SUBS[-1][1] + EXT),)
BLOCKS = ((0, 512), (512, 512), (1024, 768))
NS = len(SUBS)

F32 = jnp.float32
BF16 = jnp.bfloat16


def mo(value, by):
    return pl.multiple_of(value, by)


def nt(a, b):
    return lax.dot_general(a, b, (((1,), (1,)), ((), ())), preferred_element_type=F32)


def nn(a, b):
    return lax.dot_general(a, b, (((1,), (0,)), ((), ())), preferred_element_type=F32)


def iota(shape, axis):
    return lax.broadcasted_iota(jnp.int32, shape, axis)


def kernel(
    cache_h, new_ref, q_h, len_ref, resid_ref, vu_h, wo_h, gain_ref, router_h, ids_ref, slots_ref, wg_h, wu_h, wd_h,
    out_ref,
    cache_v, q_v, score_v, stage_v, ctx_v, arr_v, arrf_v, vu_v, val_v, wo_v, rs_in, rs_out, hid_v, tab_s, tab_v,
    ress_v, resf_v, res_v, resw_v, gain_v, rout_v, ag_v, dsp_v, d_v, wgu_v, act_s, act_v, wd_v, wdn_v, rs2_in, rs2_out,
    part_v, fin_v, fin_s,
    l_cache, l_misc, l_weights,
    s_ctx, s_tab, s_res, s_wo, s_core, s_wd, s_val, s_rs, s_ag, s_rs2, s_dsp, s_act, s_out,
    r_tab, r_res, r_wo, r_core, r_wd, r_row, r_ring, r_out,
    row_sem, all_sem,
):
    me = lax.axis_index("ep")
    c = lax.rem(me, NC)
    z = lax.rem(me // NC, NZ)
    x = me // (NC * NZ)
    dev = x * NC + c
    quad = z // CHIPS_PER

    def idx(xx, zz, cc):
        return {"ep": (xx * NZ + zz) * NC + cc}

    def wrap(zz):
        return lax.rem(zz + 2 * NZ, NZ)

    def xwrap(xx):
        return lax.rem(xx, NX)

    def send(src, dst, ssem, rsem, to):
        pltpu.make_async_remote_copy(src_ref=src, dst_ref=dst, send_sem=ssem, recv_sem=rsem, device_id=to).start()

    def arrived(ref, sem):
        pltpu.make_async_copy(ref, ref, sem).wait()

    main = c == 1
    side = c == 0

    loads = [pltpu.make_async_copy(q_h, q_v, l_misc)]
    loads += [pltpu.make_async_copy(cache_h.at[b], cache_v.at[b], l_cache.at[b]) for b in range(2)]
    for load in loads:
        load.start()

    bar = pltpu.get_barrier_semaphore()

    @pl.when(side)
    def _():
        def greet(o, carry):
            far = HALF - (o + 1) // 2
            zz = wrap(jnp.where(lax.rem(o, 2) == 1, z + far, z - far))
            for xx in range(NX):
                pl.semaphore_signal(bar, inc=1, device_id=idx(xx, zz, 1))
            return carry
        lax.fori_loop(0, NZ, greet, 0)

    @pl.when(main)
    def _():
        for xx in range(NX):
            pl.semaphore_signal(bar, inc=1, device_id=idx(xx, z, 0))
        for step in (1, -1):
            pl.semaphore_signal(bar, inc=1, device_id=idx(x, wrap(z + step), 1))

    wo_row = mo(x * VH + c * (VH // NC), VH // NC)
    gate_at = pl.ds(mo(c * UNITS, UNITS), UNITS)
    up_at = pl.ds(mo((NC + c) * UNITS, UNITS), UNITS)
    vu_at = pl.ds(mo(c * (VH // NC), VH // NC), VH // NC)
    router_copy = pltpu.make_async_copy(
        router_h.at[:, pl.ds(mo(x * DX, 128), DX)], rout_v.at[pl.ds(0, EXPERTS), :], l_weights.at[1])
    gate_copy = pltpu.make_async_copy(wg_h, wgu_v.at[:, gate_at], l_weights.at[1])
    up_copy = pltpu.make_async_copy(wu_h, wgu_v.at[:, up_at], l_weights.at[2])
    vu_copy = pltpu.make_async_copy(vu_h, vu_v.at[vu_at, :], l_weights.at[0])

    def row_start():
        @pl.when(side)
        def _():
            pl.semaphore_wait(bar, NX)
            pl.semaphore_signal(row_sem, inc=1, device_id=idx(x, z, 1))

        @pl.when(main)
        def _():
            pl.semaphore_wait(row_sem, 1)

        for xx in range(NX):
            other = jnp.logical_not(main & (x == xx))
            columns = pl.ds(xx * DX, DX)

            @pl.when(other)
            def _():
                send(wo_h.at[:, columns], wo_v.at[pl.ds(wo_row, VH // NC), :], s_wo, r_wo, idx(xx, z, 1))

            @pl.when(jnp.logical_not(other))
            def _():
                pltpu.make_async_copy(
                    wo_h.at[:, columns], wo_v.at[pl.ds(wo_row, VH // NC), :], l_weights.at[0]).start()

        @pl.when(main)
        def _():
            partner = idx(x, z, 0)
            send(vu_h, vu_v.at[vu_at, :], s_core.at[0], r_core.at[0], partner)
            send(wd_h, wdn_v, s_core.at[1], r_core.at[1], partner)
            send(wg_h, wgu_v.at[:, gate_at], s_core.at[2], r_core.at[2], partner)
            send(wu_h, wgu_v.at[:, up_at], s_core.at[3], r_core.at[3], partner)
            rout_v[...] = jnp.zeros_like(rout_v)
            router_copy.start()

        @pl.when(side)
        def _():
            vu_copy.start()
            gate_copy.start()
            up_copy.start()

    scale = 1.0 / math.sqrt(QK)
    blk = 512
    nblk = cache_v.shape[2] // blk
    loads[0].wait()
    for b in range(2):
        if b == 1:
            row_start()
        qb = q_v[b]
        qf = qb.astype(F32)
        step_of = iota((2 * H, 1), 0) // H
        new_rows = [new_ref[b, pl.ds(t, 1), :].astype(F32) for t in range(2)]
        s_new = [jnp.sum(qf * row, axis=1, keepdims=True) * scale for row in new_rows]
        s_new[1] = jnp.where(step_of >= 1, s_new[1], -jnp.inf)
        peak = jnp.maximum(s_new[0], s_new[1])
        loads[1 + b].wait()
        for p in range(nblk):
            sc = nn(qb, cache_v[b, :, pl.ds(p * blk, blk)]) * scale
            pos = iota((2 * H, blk), 1) + p * blk
            sc = jnp.where(pos < len_ref[b], sc, -jnp.inf)
            score_v[:, pl.ds(p * blk, blk)] = sc
            peak = jnp.maximum(peak, jnp.max(sc, axis=1, keepdims=True))
        p_new = [jnp.exp(s - peak) for s in s_new]
        total = p_new[0] + p_new[1]
        acc = p_new[0].astype(BF16).astype(F32) * new_rows[0][:, :LAT]
        acc = acc + p_new[1].astype(BF16).astype(F32) * new_rows[1][:, :LAT]
        for p in range(nblk):
            pr = jnp.exp(score_v[:, pl.ds(p * blk, blk)] - peak)
            total = total + jnp.sum(pr, axis=1, keepdims=True)
            acc = acc + nt(pr.astype(BF16), cache_v[b, pl.ds(0, LAT), pl.ds(p * blk, blk)])
        ctx = acc / total
        for s in range(2):
            for j in range(LAT // 128):
                stage_v[pl.ds(j * TOK + b * 2 + s, H, stride=16), :] = ctx[s * H:(s + 1) * H, j * 128:(j + 1) * 128]
    ctx_v[...] = stage_v[...].reshape(H, 16, 128).astype(BF16)

    @pl.when(main)
    def _():
        pl.semaphore_wait(bar, NX * NZ + 2)
        pl.semaphore_signal(all_sem, inc=1, device_id=idx(x, z, 0))

    @pl.when(side)
    def _():
        pl.semaphore_wait(all_sem, 1)

    def ctx_send(o, carry):
        far = HALF - (o + 1) // 2
        zz = wrap(jnp.where(lax.rem(o, 2) == 1, z + far, z - far))
        for i in range(NX):
            xx = xwrap(x + i + 1)
            own = side & (zz == z) & (xx == x)

            @pl.when(jnp.logical_not(own))
            def _():
                send(ctx_v.at[xx * NZ + zz], arr_v.at[z, dev], s_ctx, r_row.at[z], idx(xx, zz, 0))

            @pl.when(own)
            def _():
                arr_v[z, dev] = ctx_v[xx * NZ + zz]
        return carry
    lax.fori_loop(0, NZ, ctx_send, 0)

    rows8, lanes8 = iota((8, 128), 0), iota((8, 128), 1)
    table = jnp.zeros((8, 128), F32)
    for t in range(TOK):
        for k in range(TOP):
            hit = (rows8 == t) & (lanes8 == ids_ref[t // 2, t % 2, k] + LANE_TAB)
            table = jnp.where(hit, (slots_ref[t // 2, t % 2, k] + 1).astype(F32), table)
    tab_s[...] = table

    resf_v[...] = jnp.zeros_like(resf_v)
    for t in range(TOK):
        row = resid_ref[t // 2, pl.ds(t % 2, 1), :].astype(F32)
        for xx in range(NX):
            for j in range(JX):
                col = xx * DX + j * 128
                resf_v[pl.ds(xx * MSG + t * JX + j, 1), :] = row[:, col:col + 128]
    ress_v[...] = resf_v[...].reshape(NX, MSG, 128).astype(BF16)

    for xx in range(NX):
        other = jnp.logical_not(main & (x == xx))

        @pl.when(other)
        def _():
            send(tab_s, tab_v.at[dev], s_tab, r_tab, idx(xx, z, 1))
            send(ress_v.at[xx], res_v.at[dev], s_res, r_res, idx(xx, z, 1))

        @pl.when(jnp.logical_not(other))
        def _():
            tab_v[dev] = tab_s[...]
            res_v[dev] = ress_v[xx]

    def up_down(k):
        return wrap(z - k), wrap(z + k)

    @pl.when(side)
    def _side():
        vu_copy.wait()
        arrived(vu_v.at[pl.ds(0, VH // NC), :], r_core.at[0])
        own_lanes = pl.ds(mo(x * VH, VH), VH)

        def ctx_row(r):
            @pl.when(r == z)
            def _():
                arrived(arr_v.at[r, pl.ds(0, DEV - 1)], r_row.at[r])

            @pl.when(r != z)
            def _():
                arrived(arr_v.at[r], r_row.at[r])

            arrf_v[...] = arr_v[r].reshape(DEV * 16, 128).astype(F32)
            cols = []
            for j in range(LAT // 128):
                cols.append(jnp.concatenate(
                    [arrf_v[pl.ds(j * TOK + t, DEV, stride=16), :] for t in range(TOK)], axis=0))
            rows = jnp.concatenate(cols, axis=1).astype(BF16)
            val_v[r, :, own_lanes] = nt(rows, vu_v[...]).astype(BF16)
            view = val_v.at[r, :, own_lanes]
            for i in range(NX):
                send(view, view, s_val, r_row.at[r], idx(xwrap(x + i + 1), z, 1))

        def ctx_step(o, carry):
            far = HALF - (o + 1) // 2
            ctx_row(wrap(jnp.where(lax.rem(o, 2) == 1, z + far, z - far)))
            return carry
        lax.fori_loop(0, NZ, ctx_step, 0)

        arrived(wdn_v, r_core.at[1])
        for i in range(NX):
            xx = xwrap(x + i + 1)
            columns = pl.ds(mo(xx * DX, 128), DX)
            base = x * NC * UNITS
            send(wd_h.at[:, columns], wd_v.at[pl.ds(mo(base, UNITS), UNITS), :], s_wd, r_wd, idx(xx, z, 1))
            send(wdn_v.at[:, columns], wd_v.at[pl.ds(mo(base + UNITS, UNITS), UNITS), :], s_wd, r_wd, idx(xx, z, 1))

        gate_copy.wait()
        up_copy.wait()
        arrived(wgu_v.at[:, pl.ds(0, UNITS)], r_core.at[2])
        arrived(wgu_v.at[:, pl.ds(0, UNITS)], r_core.at[3])

        own_expert = x * QUAD + quad

        def experts(rows):
            for r in rows:
                arrived(d_v.at[r], r_row.at[r])
            both = jnp.zeros((SLOT * len(rows), 2 * NC * UNITS), F32)
            ext = jnp.zeros((SLOT * len(rows), EXT), F32)
            for xx in range(NX):
                both = both + nn(
                    jnp.concatenate([d_v[r, xx, :, pl.ds(0, DX)] for r in rows], axis=0),
                    wgu_v[xx * DX:(xx + 1) * DX, :])
                piece = jnp.concatenate([d_v[r, xx, :, pl.ds(DX, EXT)] for r in rows], axis=0).astype(F32)
                ext = ext + piece
            lane = iota(ext.shape, 1)
            squares = jnp.sum(
                jnp.where((lane == LANE_SUM) | (lane == LANE_SUM + 1), ext, 0.0), axis=1, keepdims=True)
            inv = lax.rsqrt(squares / D + norm_eps)
            logits = (ext + pltpu.roll(ext, EXT - EXPERTS, 1)) * inv
            named = (pltpu.roll(piece, EXT - LANE_TAB, 1) > 0.0) & (lane < EXPERTS)
            gates = jnp.where(named, 1.0 / (1.0 + jnp.exp(-logits)), 0.0)
            norm = jnp.sum(gates, axis=1, keepdims=True)
            mine = jnp.sum(jnp.where(lane == own_expert, gates, 0.0), axis=1, keepdims=True)
            share = jnp.where(norm > 0.0, route_scale * mine / norm, 0.0)
            gate = both[:, :NC * UNITS] * inv
            upward = both[:, NC * UNITS:] * inv
            act = (gate / (1.0 + jnp.exp(-gate)) * upward * share).astype(BF16)
            for i, r in enumerate(rows):
                act_s[r] = act[i * SLOT:(i + 1) * SLOT]
                for n in range(NX):
                    send(act_s.at[r], act_v.at[r, x], s_act, r_row.at[r], idx(xwrap(x + n + 1), z, 1))

        experts([z])

        def step(k, carry):
            experts(list(up_down(k)))
            return carry
        lax.fori_loop(1, HALF, step, 0)
        experts([wrap(z + HALF)])

        arrived(out_ref, r_out)
        arrived(ctx_v.at[pl.ds(0, NX * NZ - 1)], s_ctx)
        arrived(wo_v.at[pl.ds(0, NX * (VH // NC)), :], s_wo)
        arrived(tab_v.at[pl.ds(0, NX)], s_tab)
        arrived(res_v.at[pl.ds(0, NX)], s_res)
        arrived(wd_v, s_wd)
        arrived(val_v, s_val)
        arrived(act_v, s_act)

    @pl.when(main)
    def _main():
        up = idx(x, wrap(z + 1), 1)
        gain_v[...] = gain_ref[...].astype(F32)

        early = jnp.where(lax.rem(z, CUBE) == 0, 1, 0)

        def ways():
            for way in (early, 1 - early):
                yield way, idx(x, wrap(z + 1 - 2 * way), 1)

        def chain_step(in_ref, out_buf, ssem, s):
            for i, (o, w) in enumerate(SUBS):
                at = pl.ds(o, w)
                for way, to in ways():
                    r = wrap(z + (1 - 2 * way) * (HALF - s))

                    @pl.when((way == 0) | (s >= 2))
                    def _():
                        arrived(in_ref.at[way, s, :, at], r_ring.at[way, s, i])
                    total = part_v[r, :, at] + in_ref[way, s, :, at].astype(F32)
                    out_buf[way, s, :, at] = total.astype(BF16)
                    send(out_buf.at[way, s, :, at], in_ref.at[way, s + 1, :, at], ssem.at[way],
                         r_ring.at[way, s + 1, i], to)

        def chain_first(in_ref, out_buf, ssem, rows, weights):
            for o, w in BLOCKS:
                out_buf[0, 0, :, pl.ds(o, w)] = nn(rows, weights[:, o:o + w]).astype(BF16)
                for i in range(o // 256, (o + w) // 256):
                    at = pl.ds(*SUBS[i])
                    send(out_buf.at[0, 0, :, at], in_ref.at[0, 1, :, at], ssem.at[0], r_ring.at[0, 1, i], up)

        def chain_end(in_ref, o, w, i):
            at = pl.ds(o, w)
            for d in range(2):
                arrived(in_ref.at[d, HALF, :, at], r_ring.at[d, HALF, i])
            return part_v[z, :, at] + in_ref[0, HALF, :, at].astype(F32) + in_ref[1, HALF, :, at].astype(F32)

        rs_in[1, 1] = jnp.zeros((ROW, DX), BF16)
        rs2_in[1, 1] = jnp.zeros((ROW, DX), BF16)

        pltpu.make_async_copy(
            wo_h.at[:, pl.ds(0, DX)], wo_v.at[pl.ds(wo_row, VH // NC), :], l_weights.at[0]).wait()
        arrived(wo_v.at[pl.ds(0, (DEV - 1) * (VH // NC)), :], r_wo)

        def attended(rows):
            for r in rows:
                arrived(val_v.at[r], r_row.at[r])
            stacked = jnp.concatenate([val_v[r] for r in rows], axis=0)
            for o, w in BLOCKS:
                part = nn(stacked, wo_v[:, o:o + w])
                for i, r in enumerate(rows):
                    part_v[r, :, pl.ds(o, w)] = part[i * ROW:(i + 1) * ROW]

        first = wrap(z + HALF)
        arrived(val_v.at[first], r_row.at[first])
        chain_first(rs_in, rs_out, s_rs, val_v[first], wo_v)
        attended(list(up_down(HALF - 1)))

        def rs_step(s, carry):
            chain_step(rs_in, rs_out, s_rs, s)
            ahead = HALF - 1 - s

            @pl.when(ahead >= 1)
            def _():
                attended(list(up_down(ahead)))
            return carry
        lax.fori_loop(1, HALF, rs_step, 0)
        attended([z])

        arrived(res_v.at[pl.ds(0, DEV - 1)], r_res)
        arrived(tab_v.at[pl.ds(0, DEV - 1)], r_tab)
        resw_v[...] = res_v[...].reshape(DEV * MSG, 128).astype(F32)
        for j in range(JX):
            at = pl.ds(j * 128, 128)
            part_v[z, :, at] = part_v[z, :, at] + jnp.concatenate(
                [resw_v[pl.ds(t * JX + j, DEV, stride=MSG), :] for t in range(TOK)], axis=0)
        lane = iota((ROW, 128), 1)
        rows = iota((DEV, 128), 0)
        tabs = []
        for t in range(TOK):
            piece = jnp.zeros((DEV, 128), F32)
            for d in range(DEV):
                piece = jnp.where(rows == d, tab_v[d, pl.ds(t, 1), :], piece)
            tabs.append(piece)
        table_rows = jnp.concatenate(tabs, axis=0)
        router_copy.wait()

        def ag_send(r, i, way, slot):
            o, w = SUBS_AG[i]
            view = ag_v.at[r, :, pl.ds(o, w)]
            send(view, view, s_ag.at[way], r_ring.at[way, slot, i], idx(x, wrap(z + 1 - 2 * way), 1))

        def ag_wait(r, i, way, slot):
            o, w = SUBS_AG[i]
            arrived(ag_v.at[r, :, pl.ds(o, w)], r_ring.at[way, slot, i])

        sums = jnp.zeros((ROW, 1), F32)
        logits = jnp.zeros((ROW, 128), F32)
        for i, (o, w) in enumerate(SUBS):
            hidden = chain_end(rs_in, o, w, i)
            gain = jnp.concatenate(
                [gain_v[pl.ds(x * JX + j, 1), :] for j in range(o // 128, (o + w) // 128)], axis=1)
            ag_v[z, :, pl.ds(o, w)] = (hidden * gain).astype(BF16)
            if i < NS - 1:
                ag_send(z, i, 0, 1)
                ag_send(z, i, 1, 1)
            hid_v[:, pl.ds(o, w)] = hidden
            sums = sums + jnp.sum(hidden * hidden, axis=1, keepdims=True)
            logits = logits + nt(ag_v[z, :, pl.ds(o, w)], rout_v[:, pl.ds(o, w)])
        high = logits.astype(BF16).astype(F32)
        sums_high = sums.astype(BF16).astype(F32)
        ext = high + pltpu.roll(logits - high, EXPERTS, 1)
        ext = jnp.where(lane == LANE_SUM, sums_high, ext)
        ext = jnp.where(lane == LANE_SUM + 1, sums - sums_high, ext)
        ag_v[z, :, pl.ds(DX, EXT)] = (ext + table_rows).astype(BF16)
        ag_send(z, NS - 1, 0, 1)
        ag_send(z, NS - 1, 1, 1)

        def dispatch(rows):
            n = len(rows)
            size = n * NX * SLOT
            jj, lane = iota((size, 128), 0), iota((size, 128), 1)
            wanted_lane = LANE_TAB + lax.rem(jj // SLOT, NX) * QUAD + quad
            pick = jnp.where(lane == wanted_lane, 1.0, 0.0).astype(BF16)
            picked = nt(pick, jnp.concatenate([ag_v[r, :, pl.ds(DX, EXT)] for r in rows], axis=0))
            jj, tok = iota((size, n * ROW), 0), iota((size, n * ROW), 1)
            wanted = (lax.rem(jj, SLOT) // DEV + 1).astype(F32)
            hit = (picked == wanted) & (lax.rem(jj, DEV) == lax.rem(tok, DEV)) & (jj // (NX * SLOT) == tok // ROW)
            place = jnp.where(hit, 1.0, 0.0).astype(BF16)
            moved = nn(place, jnp.concatenate([ag_v[r] for r in rows], axis=0)).astype(BF16)
            for i, r in enumerate(rows):
                dsp_v[r] = moved[i * NX * SLOT:(i + 1) * NX * SLOT].reshape(NX, SLOT, DC)
            for r in rows:
                for i in range(NX):
                    xx = xwrap(x + i + 1)
                    send(dsp_v.at[r, xx], d_v.at[r, x], s_dsp, r_row.at[r], idx(xx, z, 0))

        def returned(rows):
            n = len(rows)
            for r in rows:
                arrived(act_v.at[r], r_row.at[r])
            size = n * NX * SLOT
            jj, lane = iota((size, 128), 0), iota((size, 128), 1)
            wanted_lane = LANE_TAB + jj // (n * SLOT) * QUAD + quad
            pick = jnp.where(lane == wanted_lane, 1.0, 0.0).astype(BF16)
            picked = nt(jnp.concatenate([ag_v[r, :, pl.ds(DX, EXT)] for r in rows], axis=0), pick)
            jj, tok = iota((n * ROW, size), 1), iota((n * ROW, size), 0)
            wanted = (lax.rem(jj, SLOT) // DEV + 1).astype(F32)
            hit = (picked == wanted) & (lax.rem(jj, DEV) == lax.rem(tok, DEV)) & (
                lax.rem(jj // SLOT, n) == tok // ROW)
            place = jnp.where(hit, 1.0, 0.0).astype(BF16)
            spread = []
            for i in range(NX):
                acts = jnp.concatenate([act_v[r, i] for r in rows], axis=0)
                spread.append(nn(place[:, i * n * SLOT:(i + 1) * n * SLOT], acts).astype(BF16))
            return jnp.concatenate(spread, axis=1)

        def down_part(rows):
            spread = returned(rows)
            for o, w in BLOCKS:
                part = nn(spread, wd_v[:, o:o + w])
                for i, r in enumerate(rows):
                    part_v[r, :, pl.ds(o, w)] = part[i * ROW:(i + 1) * ROW]

        dispatch([z])

        def ag_step(k, carry):
            for i in range(NS):
                for way, _ in ways():
                    r = wrap(z - (1 - 2 * way) * k)
                    ag_wait(r, i, way, k)

                    @pl.when((way == 0) | (k < HALF - 1))
                    def _():
                        ag_send(r, i, way, k + 1)
            dispatch(list(up_down(k)))
            return carry
        lax.fori_loop(1, HALF, ag_step, 0)
        last = wrap(z + HALF)
        for i in range(NS):
            ag_wait(last, i, 0, HALF)
        dispatch([last])

        arrived(wd_v, r_wd)
        down_part([z, *up_down(1)])

        def late(g, carry):
            down_part([*up_down(2 * g), *up_down(2 * g + 1)])
            return carry
        lax.fori_loop(1, HALF // 2, late, 0)

        spread = returned([last])
        chain_first(rs2_in, rs2_out, s_rs2, spread, wd_v)

        def rs2_step(s, carry):
            chain_step(rs2_in, rs2_out, s_rs2, s)
            return carry
        lax.fori_loop(1, HALF, rs2_step, 0)

        for t in range(TOK * JX, MSG):
            fin_v[pl.ds(t, DEV, stride=MSG), :] = jnp.zeros((DEV, 128), F32)
        for i, (o, w) in enumerate(SUBS):
            mixed = chain_end(rs2_in, o, w, i) + hid_v[:, pl.ds(o, w)]
            for t in range(TOK):
                for j in range(o // 128, (o + w) // 128):
                    fin_v[pl.ds(t * JX + j, DEV, stride=MSG), :] = (
                        mixed[t * DEV:(t + 1) * DEV, j * 128 - o:j * 128 - o + 128])
        fin_s[...] = fin_v[...].reshape(DEV, MSG, 128).astype(BF16)
        for i in range(DEV - 1):
            to = lax.rem(dev + i + 1, DEV)
            send(fin_s.at[to], out_ref.at[x], s_out, r_out, idx(to // NC, z, lax.rem(to, NC)))
        out_ref[x] = fin_s[dev]

        arrived(ctx_v, s_ctx)
        arrived(wo_v.at[pl.ds(0, (NX - 1) * (VH // NC)), :], s_wo)
        arrived(tab_v.at[pl.ds(0, NX - 1)], s_tab)
        arrived(res_v.at[pl.ds(0, NX - 1)], s_res)
        arrived(vu_v.at[pl.ds(0, VH // NC), :], s_core.at[0])
        arrived(wdn_v, s_core.at[1])
        arrived(wgu_v.at[:, pl.ds(0, UNITS)], s_core.at[2])
        arrived(wgu_v.at[:, pl.ds(0, UNITS)], s_core.at[3])
        for buf, sem in ((rs_out, s_rs), (rs2_out, s_rs2)):
            arrived(buf.at[0], sem.at[0])
            arrived(buf.at[1, pl.ds(1, HALF - 1)], sem.at[1])
        arrived(ag_v.at[pl.ds(0, HALF)], s_ag.at[0])
        arrived(ag_v.at[pl.ds(0, HALF - 1)], s_ag.at[1])
        arrived(dsp_v, s_dsp)
        arrived(fin_s.at[pl.ds(0, DEV - 1)], s_out)
        arrived(out_ref.at[pl.ds(0, NX - 1)], r_out)


def body(
    cache_kv, new_kv, queries, lengths, resid, value_up, out_proj, norm_gain, router, expert_ids, slots, w_gate, w_up,
    w_down,
):
    seqs, steps = resid.shape[:2]
    cache_len = cache_kv.shape[1]
    hbm = pl.BlockSpec(memory_space=pltpu.HBM)
    vmem = pl.BlockSpec(memory_space=pltpu.VMEM)
    smem = pl.BlockSpec(memory_space=pltpu.SMEM)
    dma = pltpu.SemaphoreType.DMA
    regular = pltpu.SemaphoreType.REGULAR
    scratch = [
        pltpu.VMEM((seqs, KV, cache_len), BF16),
        pltpu.VMEM((seqs, steps * H, KV), BF16),
        pltpu.VMEM((steps * H, cache_len), F32),
        pltpu.VMEM((H * 16, 128), F32),
        pltpu.VMEM((H, 16, 128), BF16),
        pltpu.VMEM((NZ, DEV, 16, 128), BF16),
        pltpu.VMEM((DEV * 16, 128), F32),
        pltpu.VMEM((VH, LAT), BF16),
        pltpu.VMEM((NZ, ROW, NX * VH), BF16),
        pltpu.VMEM((NX * VH, DX), BF16),
        pltpu.VMEM((2, HALF + 1, ROW, DX), BF16),
        pltpu.VMEM((2, HALF, ROW, DX), BF16),
        pltpu.VMEM((ROW, DX), F32),
        pltpu.VMEM((8, 128), F32),
        pltpu.VMEM((DEV, 8, 128), F32),
        pltpu.VMEM((NX, MSG, 128), BF16),
        pltpu.VMEM((NX * MSG, 128), F32),
        pltpu.VMEM((DEV, MSG, 128), BF16),
        pltpu.VMEM((DEV * MSG, 128), F32),
        pltpu.VMEM((D // 128, 128), F32),
        pltpu.VMEM((128, DX), BF16),
        pltpu.VMEM((NZ, ROW, DC), BF16),
        pltpu.VMEM((NZ, NX, SLOT, DC), BF16),
        pltpu.VMEM((NZ, NX, SLOT, DC), BF16),
        pltpu.VMEM((D, 2 * NC * UNITS), BF16),
        pltpu.VMEM((NZ, SLOT, NC * UNITS), BF16),
        pltpu.VMEM((NZ, NX, SLOT, NC * UNITS), BF16),
        pltpu.VMEM((NX * NC * UNITS, DX), BF16),
        pltpu.VMEM((UNITS, D), BF16),
        pltpu.VMEM((2, HALF + 1, ROW, DX), BF16),
        pltpu.VMEM((2, HALF, ROW, DX), BF16),
        pltpu.VMEM((NZ, ROW, DX), F32),
        pltpu.VMEM((DEV * MSG, 128), F32),
        pltpu.VMEM((DEV, MSG, 128), BF16),
        dma((seqs,)), dma, dma((3,)),
        dma, dma, dma, dma, dma((4,)), dma, dma, dma((2,)), dma((2,)), dma((2,)), dma, dma, dma,
        dma, dma, dma, dma((4,)), dma, dma((NZ,)), dma((2, HALF + 1, NS)), dma,
        regular, regular,
    ]
    out = pl.pallas_call(
        kernel,
        out_shape=jax.ShapeDtypeStruct((NX, MSG, 128), BF16),
        in_specs=[hbm, vmem, hbm, smem, vmem, hbm, hbm, vmem, hbm, smem, smem, hbm, hbm, hbm],
        out_specs=vmem,
        scratch_shapes=scratch,
        compiler_params=pltpu.CompilerParams(
            collective_id=0, has_side_effects=True, vmem_limit_bytes=(64 << 20) - (64 << 10)),
        name="layer",
    )(
        jnp.transpose(cache_kv, (0, 2, 1)), new_kv, queries.reshape(seqs, steps * H, KV), lengths, resid,
        value_up.T, out_proj, norm_gain.reshape(D // 128, 128), router.T, expert_ids, slots, w_gate, w_up, w_down,
    )
    out = out[:, :TOK * JX].reshape(NX, TOK, JX, 128).transpose(1, 0, 2, 3)
    return out.reshape(resid.shape)


def solution(mesh):
    return jax.shard_map(
        body,
        mesh=mesh,
        in_specs=(
            P(("rep", "ep"), None, None),
            P(("rep", "ep"), None, None),
            P(("rep", "ep"), None, None, None),
            P(("rep", "ep")),
            P(("rep", "ep"), None, None),
            P(None, "ep"),
            P("ep", None),
            P(),
            P(),
            P(("rep", "ep"), None, None),
            P(("rep", "ep"), None, None),
            P(None, "ep"),
            P(None, "ep"),
            P("ep", None),
        ),
        out_specs=P(("rep", "ep"), None, None),
        check_vma=False,
    )
```

time: 146 us -> 123 us (0.84)
  Pallas kernels: 143 us -> 122 us
    pallas_call x1, Pallas kernels: 143 us -> 122 us  [body(): pl.pallas_call(kernel, out_shape=jax.ShapeDtypeStruct((NX, MSG, 128), BF1...]
where the time goes in v2:
time: 123 us
  Pallas kernels  122 us (99%)
  local copies, waits for them, and re-layouts  1.52 us (1%)
    pallas_call x1, Pallas kernels, body(): pl.pallas_call(kernel, out_shape=jax.ShapeDtypeStruct((NX, MSG, 128), BF1...  122 us

profile of v2, /device:TPU:33, one launch (start us, length us, event | category | flops | bytes accessed | tf_op | source)
XLA Modules:
  0.0 123.1 jit_solution(11321348387155198152)
XLA Ops:
  0.0 121.6 %layer.1 = bf16[4,64,128]{2,1,0:T(8,128)(2,1)} custom-call(bf16[2,576,2048]{2,1,0:T(8,128)(2,1)} %bitcast.8, bf16[2,2,576]{2,1,0:T(2,128)(2,1)} %new_ref.1, bf16[2,128,576]{2,1,0:T(8,128)(2,1)} %bitcast.9, s32[2]{0:T(128)} %len_ref.1, bf16[2,2,7168]{2,1,0:T(2,128)(2,1)} %resid_ref.1, bf16[64,512]{1,0:T(8,128)(2,1)} %bitcast.12, bf16[64,7168]{1,0:T(8,128)(2,1)} %wo_h.1, ...), custom_call_target="tpu_custom_call" | custom-call | tf_op jit(solution)/shard_map/layer/pallas_call | solution.py:647
  121.6 0.8 slice.3
  122.5 0.7 reshape.15
  (2 shorter events, 0.0 us)

commit v3 on v2

--- a/solution.py
+++ b/solution.py
@@ -27,7 +27,6 @@
 SLOT = DEV * CAP
 DX = D // NX
 EXT = 128
-DC = DX + EXT
 JX = DX // 128
 MSG = 64
 LANE_SUM = 32
@@ -40,10 +39,16 @@
 
 CUBE = 4
 
-SUBS = tuple((256 * i, 256) for i in range(DX // 256))
-SUBS_AG = SUBS[:-1] + ((SUBS[-1][0], SUBS[-1][1] + EXT),)
+BX = 384
+DA = DX - BX
+DAE = DA + EXT
+DG = DAE + NX * BX
+PIECE = 384
+SUBS = ((DA, BX),) + tuple((o, min(PIECE, DA - o)) for o in range(0, DA, PIECE))
+NS = len(SUBS)
+NP = DG // PIECE
+NPA = DAE // PIECE
 BLOCKS = ((0, 512), (512, 512), (1024, 768))
-NS = len(SUBS)
 
 F32 = jnp.float32
 BF16 = jnp.bfloat16
@@ -66,14 +71,15 @@
 
 
 def kernel(
-    cache_h, new_ref, q_h, len_ref, resid_ref, vu_h, wo_h, gain_ref, router_h, ids_ref, slots_ref, wg_h, wu_h, wd_h,
+    cache_h, new_h, q_h, len_h, resid_h, vu_h, wo_h, gain_h, router_h, ids_h, slots_h, wg_h, wu_h, wd_h,
     out_ref,
+    new_ref, len_ref, resid_ref, gain_ref, ids_ref, slots_ref,
     cache_v, q_v, score_v, stage_v, ctx_v, arr_v, arrf_v, vu_v, val_v, wo_v, rs_in, rs_out, hid_v, tab_s, tab_v,
     ress_v, resf_v, res_v, resw_v, gain_v, rout_v, ag_v, dsp_v, d_v, wgu_v, act_s, act_v, wd_v, wdn_v, rs2_in, rs2_out,
     part_v, fin_v, fin_s,
-    l_cache, l_misc, l_weights,
-    s_ctx, s_tab, s_res, s_wo, s_core, s_wd, s_val, s_rs, s_ag, s_rs2, s_dsp, s_act, s_out,
-    r_tab, r_res, r_wo, r_core, r_wd, r_row, r_ring, r_out,
+    l_cache, l_misc, l_weights, l_small,
+    s_ctx, s_tab, s_res, s_wo, s_core, s_wd, s_val, s_rs, s_ag, s_rs2, s_dsp, s_act, s_out, s_bx,
+    r_tab, r_res, r_wo, r_core, r_wd, r_row, r_ring, r_out, r_bx, r_twin,
     row_sem, all_sem,
 ):
     me = lax.axis_index("ep")
@@ -82,6 +88,9 @@
     x = me // (NC * NZ)
     dev = x * NC + c
     quad = z // CHIPS_PER
+    group = lax.axis_index("rep")
+    half = lax.rem(group, 2)
+    twin = {"rep": group + 1 - 2 * half, "ep": me}
 
     def idx(xx, zz, cc):
         return {"ep": (xx * NZ + zz) * NC + cc}
@@ -103,7 +112,12 @@
 
     loads = [pltpu.make_async_copy(q_h, q_v, l_misc)]
     loads += [pltpu.make_async_copy(cache_h.at[b], cache_v.at[b], l_cache.at[b]) for b in range(2)]
-    for load in loads:
+    small = [
+        pltpu.make_async_copy(src, dst, l_small.at[i]) for i, (src, dst) in enumerate((
+            (new_h, new_ref), (len_h, len_ref), (resid_h, resid_ref), (gain_h, gain_ref), (ids_h, ids_ref),
+            (slots_h, slots_ref)))
+    ]
+    for load in loads[:2] + small[:2] + loads[2:] + small[2:]:
         load.start()
 
     bar = pltpu.get_barrier_semaphore()
@@ -124,8 +138,8 @@
             pl.semaphore_signal(bar, inc=1, device_id=idx(xx, z, 0))
         for step in (1, -1):
             pl.semaphore_signal(bar, inc=1, device_id=idx(x, wrap(z + step), 1))
-
-    wo_row = mo(x * VH + c * (VH // NC), VH // NC)
+        pl.semaphore_signal(bar, inc=1, device_id=twin)
+
     gate_at = pl.ds(mo(c * UNITS, UNITS), UNITS)
     up_at = pl.ds(mo((NC + c) * UNITS, UNITS), UNITS)
     vu_at = pl.ds(mo(c * (VH // NC), VH // NC), VH // NC)
@@ -135,6 +149,19 @@
     up_copy = pltpu.make_async_copy(wu_h, wgu_v.at[:, up_at], l_weights.at[2])
     vu_copy = pltpu.make_async_copy(vu_h, vu_v.at[vu_at, :], l_weights.at[0])
 
+    wo_row = pl.ds(mo(x * VH + c * (VH // NC), VH // NC), VH // NC)
+
+    def own_columns(xx):
+        return pl.ds(mo(xx * DX, 128), DX)
+
+    wo_copy = pltpu.make_async_copy(wo_h.at[:, own_columns(x)], wo_v.at[wo_row, :], l_weights.at[0])
+
+    def wo_send(xx):
+        send(wo_h.at[:, own_columns(xx)], wo_v.at[wo_row, :], s_wo, r_wo, idx(xx, z, 1))
+
+    def wd_rows(xx, cc):
+        return pl.ds(mo((xx * NC + cc) * UNITS, UNITS), UNITS)
+
     def row_start():
         @pl.when(side)
         def _():
@@ -145,39 +172,27 @@
         def _():
             pl.semaphore_wait(row_sem, 1)
 
-        for xx in range(NX):
-            other = jnp.logical_not(main & (x == xx))
-            columns = pl.ds(xx * DX, DX)
-
-            @pl.when(other)
-            def _():
-                send(wo_h.at[:, columns], wo_v.at[pl.ds(wo_row, VH // NC), :], s_wo, r_wo, idx(xx, z, 1))
-
-            @pl.when(jnp.logical_not(other))
-            def _():
-                pltpu.make_async_copy(
-                    wo_h.at[:, columns], wo_v.at[pl.ds(wo_row, VH // NC), :], l_weights.at[0]).start()
+        for i in range(NX - 1):
+            wo_send(xwrap(x + i + 1))
 
         @pl.when(main)
         def _():
-            partner = idx(x, z, 0)
-            send(vu_h, vu_v.at[vu_at, :], s_core.at[0], r_core.at[0], partner)
-            send(wd_h, wdn_v, s_core.at[1], r_core.at[1], partner)
-            send(wg_h, wgu_v.at[:, gate_at], s_core.at[2], r_core.at[2], partner)
-            send(wu_h, wgu_v.at[:, up_at], s_core.at[3], r_core.at[3], partner)
+            wo_copy.start()
+            send(vu_h, vu_v.at[vu_at, :], s_core.at[0], r_core.at[0], idx(x, z, 0))
             rout_v[...] = jnp.zeros_like(rout_v)
             router_copy.start()
 
         @pl.when(side)
         def _():
+            wo_send(x)
             vu_copy.start()
-            gate_copy.start()
-            up_copy.start()
 
     scale = 1.0 / math.sqrt(QK)
     blk = 512
     nblk = cache_v.shape[2] // blk
     loads[0].wait()
+    small[0].wait()
+    small[1].wait()
     for b in range(2):
         if b == 1:
             row_start()
@@ -211,7 +226,7 @@
 
     @pl.when(main)
     def _():
-        pl.semaphore_wait(bar, NX * NZ + 2)
+        pl.semaphore_wait(bar, NX * NZ + 3)
         pl.semaphore_signal(all_sem, inc=1, device_id=idx(x, z, 0))
 
     @pl.when(side)
@@ -234,6 +249,22 @@
                 arr_v[z, dev] = ctx_v[xx * NZ + zz]
         return carry
     lax.fori_loop(0, NZ, ctx_send, 0)
+
+    @pl.when(main)
+    def _():
+        @pl.when(half == 1)
+        def _():
+            send(wd_h, wdn_v, s_core.at[1], r_core.at[1], idx(x, z, 0))
+        send(wg_h, wgu_v.at[:, gate_at], s_core.at[2], r_core.at[2], idx(x, z, 0))
+        send(wu_h, wgu_v.at[:, up_at], s_core.at[3], r_core.at[3], idx(x, z, 0))
+
+    @pl.when(side)
+    def _():
+        gate_copy.start()
+        up_copy.start()
+
+    for load in small[2:]:
+        load.wait()
 
     rows8, lanes8 = iota((8, 128), 0), iota((8, 128), 1)
     table = jnp.zeros((8, 128), F32)
@@ -273,6 +304,11 @@
         vu_copy.wait()
         arrived(vu_v.at[pl.ds(0, VH // NC), :], r_core.at[0])
         own_lanes = pl.ds(mo(x * VH, VH), VH)
+
+        def wd_send(source):
+            for i in range(NX):
+                xx = xwrap(x + i + 1)
+                send(source.at[:, own_columns(xx)], wd_v.at[wd_rows(x, half), :], s_wd, r_wd, idx(xx, z, 1))
 
         def ctx_row(r):
             @pl.when(r == z)
@@ -300,13 +336,14 @@
             return carry
         lax.fori_loop(0, NZ, ctx_step, 0)
 
-        arrived(wdn_v, r_core.at[1])
-        for i in range(NX):
-            xx = xwrap(x + i + 1)
-            columns = pl.ds(mo(xx * DX, 128), DX)
-            base = x * NC * UNITS
-            send(wd_h.at[:, columns], wd_v.at[pl.ds(mo(base, UNITS), UNITS), :], s_wd, r_wd, idx(xx, z, 1))
-            send(wdn_v.at[:, columns], wd_v.at[pl.ds(mo(base + UNITS, UNITS), UNITS), :], s_wd, r_wd, idx(xx, z, 1))
+        @pl.when(half == 0)
+        def _():
+            wd_send(wd_h)
+
+        @pl.when(half == 1)
+        def _():
+            arrived(wdn_v, r_core.at[1])
+            wd_send(wdn_v)
 
         gate_copy.wait()
         up_copy.wait()
@@ -320,11 +357,13 @@
                 arrived(d_v.at[r], r_row.at[r])
             both = jnp.zeros((SLOT * len(rows), 2 * NC * UNITS), F32)
             ext = jnp.zeros((SLOT * len(rows), EXT), F32)
+            shared = jnp.concatenate([d_v[r, NX] for r in rows], axis=0)
             for xx in range(NX):
                 both = both + nn(
-                    jnp.concatenate([d_v[r, xx, :, pl.ds(0, DX)] for r in rows], axis=0),
-                    wgu_v[xx * DX:(xx + 1) * DX, :])
-                piece = jnp.concatenate([d_v[r, xx, :, pl.ds(DX, EXT)] for r in rows], axis=0).astype(F32)
+                    jnp.concatenate([d_v[r, xx, :, pl.ds(0, DA)] for r in rows], axis=0),
+                    wgu_v[xx * DX:xx * DX + DA, :])
+                both = both + nn(shared[:, xx * BX:(xx + 1) * BX], wgu_v[xx * DX + DA:(xx + 1) * DX, :])
+                piece = jnp.concatenate([d_v[r, xx, :, pl.ds(DA, EXT)] for r in rows], axis=0).astype(F32)
                 ext = ext + piece
             lane = iota(ext.shape, 1)
             squares = jnp.sum(
@@ -357,7 +396,7 @@
         arrived(wo_v.at[pl.ds(0, NX * (VH // NC)), :], s_wo)
         arrived(tab_v.at[pl.ds(0, NX)], s_tab)
         arrived(res_v.at[pl.ds(0, NX)], s_res)
-        arrived(wd_v, s_wd)
+        arrived(wd_v.at[pl.ds(0, NX * UNITS), :], s_wd)
         arrived(val_v, s_val)
         arrived(act_v, s_act)
 
@@ -366,44 +405,53 @@
         up = idx(x, wrap(z + 1), 1)
         gain_v[...] = gain_ref[...].astype(F32)
 
-        early = jnp.where(lax.rem(z, CUBE) == 0, 1, 0)
-
-        def ways():
-            for way in (early, 1 - early):
-                yield way, idx(x, wrap(z + 1 - 2 * way), 1)
-
-        def chain_step(in_ref, out_buf, ssem, s):
+        early = jnp.where(lax.rem(z, CUBE) < CUBE // 2, 1, 0)
+
+        def ways(pieces):
+            for i in range(pieces + 1):
+                if i < pieces:
+                    yield i, early, idx(x, wrap(z + 1 - 2 * early), 1)
+                if i > 0:
+                    yield i - 1, 1 - early, idx(x, wrap(z - 1 + 2 * early), 1)
+
+        def slot_a(s):
+            return lax.rem(s, 3)
+
+        def slot_g(k):
+            return lax.rem(k + 2, 3)
+
+        def slot_b(s):
+            return jnp.where(s <= 3, s + 2, lax.rem(s, 3))
+
+        def chain_step(in_ref, out_buf, ssem, slot, s):
+            for i, way, to in ways(NS):
+                at = pl.ds(*SUBS[i])
+                r = wrap(z + (1 - 2 * way) * (HALF - s))
+
+                @pl.when((way == 0) | (s >= 2))
+                def _():
+                    arrived(in_ref.at[way, s, :, at], r_ring.at[way, slot(s), i])
+                total = part_v[r, :, at] + in_ref[way, s, :, at].astype(F32)
+                out_buf[way, s, :, at] = total.astype(BF16)
+                send(out_buf.at[way, s, :, at], in_ref.at[way, s + 1, :, at], ssem.at[way],
+                     r_ring.at[way, slot(s + 1), i], to)
+
+        def chain_first(in_ref, out_buf, ssem, slot, rows, weights):
             for i, (o, w) in enumerate(SUBS):
                 at = pl.ds(o, w)
-                for way, to in ways():
-                    r = wrap(z + (1 - 2 * way) * (HALF - s))
-
-                    @pl.when((way == 0) | (s >= 2))
-                    def _():
-                        arrived(in_ref.at[way, s, :, at], r_ring.at[way, s, i])
-                    total = part_v[r, :, at] + in_ref[way, s, :, at].astype(F32)
-                    out_buf[way, s, :, at] = total.astype(BF16)
-                    send(out_buf.at[way, s, :, at], in_ref.at[way, s + 1, :, at], ssem.at[way],
-                         r_ring.at[way, s + 1, i], to)
-
-        def chain_first(in_ref, out_buf, ssem, rows, weights):
-            for o, w in BLOCKS:
-                out_buf[0, 0, :, pl.ds(o, w)] = nn(rows, weights[:, o:o + w]).astype(BF16)
-                for i in range(o // 256, (o + w) // 256):
-                    at = pl.ds(*SUBS[i])
-                    send(out_buf.at[0, 0, :, at], in_ref.at[0, 1, :, at], ssem.at[0], r_ring.at[0, 1, i], up)
-
-        def chain_end(in_ref, o, w, i):
+                out_buf[0, 0, :, at] = nn(rows, weights[:, o:o + w]).astype(BF16)
+                send(out_buf.at[0, 0, :, at], in_ref.at[0, 1, :, at], ssem.at[0], r_ring.at[0, slot(1), i], up)
+
+        def chain_end(in_ref, slot, o, w, i):
             at = pl.ds(o, w)
             for d in range(2):
-                arrived(in_ref.at[d, HALF, :, at], r_ring.at[d, HALF, i])
+                arrived(in_ref.at[d, HALF, :, at], r_ring.at[d, slot(HALF), i])
             return part_v[z, :, at] + in_ref[0, HALF, :, at].astype(F32) + in_ref[1, HALF, :, at].astype(F32)
 
         rs_in[1, 1] = jnp.zeros((ROW, DX), BF16)
         rs2_in[1, 1] = jnp.zeros((ROW, DX), BF16)
 
-        pltpu.make_async_copy(
-            wo_h.at[:, pl.ds(0, DX)], wo_v.at[pl.ds(wo_row, VH // NC), :], l_weights.at[0]).wait()
+        wo_copy.wait()
         arrived(wo_v.at[pl.ds(0, (DEV - 1) * (VH // NC)), :], r_wo)
 
         def attended(rows):
@@ -417,11 +465,11 @@
 
         first = wrap(z + HALF)
         arrived(val_v.at[first], r_row.at[first])
-        chain_first(rs_in, rs_out, s_rs, val_v[first], wo_v)
+        chain_first(rs_in, rs_out, s_rs, slot_a, val_v[first], wo_v)
         attended(list(up_down(HALF - 1)))
 
         def rs_step(s, carry):
-            chain_step(rs_in, rs_out, s_rs, s)
+            chain_step(rs_in, rs_out, s_rs, slot_a, s)
             ahead = HALF - 1 - s
 
             @pl.when(ahead >= 1)
@@ -449,55 +497,73 @@
         table_rows = jnp.concatenate(tabs, axis=0)
         router_copy.wait()
 
-        def ag_send(r, i, way, slot):
-            o, w = SUBS_AG[i]
-            view = ag_v.at[r, :, pl.ds(o, w)]
-            send(view, view, s_ag.at[way], r_ring.at[way, slot, i], idx(x, wrap(z + 1 - 2 * way), 1))
-
-        def ag_wait(r, i, way, slot):
-            o, w = SUBS_AG[i]
-            arrived(ag_v.at[r, :, pl.ds(o, w)], r_ring.at[way, slot, i])
+        def ag_send(r, i, way, k):
+            view = ag_v.at[r, :, pl.ds(i * PIECE, PIECE)]
+            send(view, view, s_ag.at[way], r_ring.at[way, slot_g(k), i], idx(x, wrap(z + 1 - 2 * way), 1))
+
+        def ag_wait(r, i, way, k):
+            arrived(ag_v.at[r, :, pl.ds(i * PIECE, PIECE)], r_ring.at[way, slot_g(k), i])
 
         sums = jnp.zeros((ROW, 1), F32)
         logits = jnp.zeros((ROW, 128), F32)
+        bx_at = pl.ds(mo(DAE + x * BX, 128), BX)
         for i, (o, w) in enumerate(SUBS):
-            hidden = chain_end(rs_in, o, w, i)
+            hidden = chain_end(rs_in, slot_a, o, w, i)
             gain = jnp.concatenate(
                 [gain_v[pl.ds(x * JX + j, 1), :] for j in range(o // 128, (o + w) // 128)], axis=1)
-            ag_v[z, :, pl.ds(o, w)] = (hidden * gain).astype(BF16)
-            if i < NS - 1:
-                ag_send(z, i, 0, 1)
-                ag_send(z, i, 1, 1)
+            scaled = (hidden * gain).astype(BF16)
+            if i == 0:
+                ag_v[z, :, bx_at] = scaled
+                view = ag_v.at[z, :, bx_at]
+                for j in range(NX - 1):
+                    send(view, view, s_bx, r_bx, idx(xwrap(x + j + 1), z, 1))
+            else:
+                ag_v[z, :, pl.ds(o, w)] = scaled
+                if i < NS - 1:
+                    ag_send(z, i - 1, 0, 1)
+                    ag_send(z, i - 1, 1, 1)
             hid_v[:, pl.ds(o, w)] = hidden
             sums = sums + jnp.sum(hidden * hidden, axis=1, keepdims=True)
-            logits = logits + nt(ag_v[z, :, pl.ds(o, w)], rout_v[:, pl.ds(o, w)])
+            logits = logits + nt(scaled, rout_v[:, pl.ds(o, w)])
         high = logits.astype(BF16).astype(F32)
         sums_high = sums.astype(BF16).astype(F32)
         ext = high + pltpu.roll(logits - high, EXPERTS, 1)
         ext = jnp.where(lane == LANE_SUM, sums_high, ext)
         ext = jnp.where(lane == LANE_SUM + 1, sums - sums_high, ext)
-        ag_v[z, :, pl.ds(DX, EXT)] = (ext + table_rows).astype(BF16)
-        ag_send(z, NS - 1, 0, 1)
-        ag_send(z, NS - 1, 1, 1)
+        ag_v[z, :, pl.ds(DA, EXT)] = (ext + table_rows).astype(BF16)
+        ag_send(z, NPA - 1, 0, 1)
+        ag_send(z, NPA - 1, 1, 1)
+        arrived(wd_v.at[pl.ds(0, NX * UNITS), :], r_wd)
+        for xx in range(NX):
+            view = wd_v.at[wd_rows(xx, half), :]
+            send(view, view, s_wd, r_twin, twin)
+        arrived(ag_v.at[z, :, pl.ds(DAE, (NX - 1) * BX)], r_bx)
+        for i in range(NPA, NP):
+            ag_send(z, i, 0, 1)
+            ag_send(z, i, 1, 1)
 
         def dispatch(rows):
             n = len(rows)
             size = n * NX * SLOT
             jj, lane = iota((size, 128), 0), iota((size, 128), 1)
-            wanted_lane = LANE_TAB + lax.rem(jj // SLOT, NX) * QUAD + quad
+            wanted_lane = LANE_TAB + lax.rem(x + lax.rem(jj // SLOT, NX), NX) * QUAD + quad
             pick = jnp.where(lane == wanted_lane, 1.0, 0.0).astype(BF16)
-            picked = nt(pick, jnp.concatenate([ag_v[r, :, pl.ds(DX, EXT)] for r in rows], axis=0))
+            picked = nt(pick, jnp.concatenate([ag_v[r, :, pl.ds(DA, EXT)] for r in rows], axis=0))
             jj, tok = iota((size, n * ROW), 0), iota((size, n * ROW), 1)
             wanted = (lax.rem(jj, SLOT) // DEV + 1).astype(F32)
             hit = (picked == wanted) & (lax.rem(jj, DEV) == lax.rem(tok, DEV)) & (jj // (NX * SLOT) == tok // ROW)
             place = jnp.where(hit, 1.0, 0.0).astype(BF16)
-            moved = nn(place, jnp.concatenate([ag_v[r] for r in rows], axis=0)).astype(BF16)
+            moved = nn(place, jnp.concatenate([ag_v[r, :, pl.ds(0, DAE)] for r in rows], axis=0)).astype(BF16)
+            own = jnp.concatenate([place[i * NX * SLOT:i * NX * SLOT + SLOT] for i in range(n)], axis=0)
+            shared = nn(own, jnp.concatenate([ag_v[r, :, pl.ds(DAE, NX * BX)] for r in rows], axis=0)).astype(BF16)
             for i, r in enumerate(rows):
-                dsp_v[r] = moved[i * NX * SLOT:(i + 1) * NX * SLOT].reshape(NX, SLOT, DC)
+                dsp_v[r, pl.ds(0, NX)] = moved[i * NX * SLOT:(i + 1) * NX * SLOT].reshape(NX, SLOT, DAE)
+                dsp_v[r, NX] = shared[i * SLOT:(i + 1) * SLOT]
             for r in rows:
-                for i in range(NX):
-                    xx = xwrap(x + i + 1)
-                    send(dsp_v.at[r, xx], d_v.at[r, x], s_dsp, r_row.at[r], idx(xx, z, 0))
+                for i in range(1, NX):
+                    send(dsp_v.at[r, i], d_v.at[r, x], s_dsp, r_row.at[r], idx(xwrap(x + i), z, 0))
+                send(dsp_v.at[r, 0], d_v.at[r, x], s_dsp, r_row.at[r], idx(x, z, 0))
+                send(dsp_v.at[r, NX], d_v.at[r, NX], s_dsp, r_row.at[r], idx(x, z, 0))
 
         def returned(rows):
             n = len(rows)
@@ -507,7 +573,7 @@
             jj, lane = iota((size, 128), 0), iota((size, 128), 1)
             wanted_lane = LANE_TAB + jj // (n * SLOT) * QUAD + quad
             pick = jnp.where(lane == wanted_lane, 1.0, 0.0).astype(BF16)
-            picked = nt(jnp.concatenate([ag_v[r, :, pl.ds(DX, EXT)] for r in rows], axis=0), pick)
+            picked = nt(jnp.concatenate([ag_v[r, :, pl.ds(DA, EXT)] for r in rows], axis=0), pick)
             jj, tok = iota((n * ROW, size), 1), iota((n * ROW, size), 0)
             wanted = (lax.rem(jj, SLOT) // DEV + 1).astype(F32)
             hit = (picked == wanted) & (lax.rem(jj, DEV) == lax.rem(tok, DEV)) & (
@@ -529,23 +595,22 @@
         dispatch([z])
 
         def ag_step(k, carry):
-            for i in range(NS):
-                for way, _ in ways():
-                    r = wrap(z - (1 - 2 * way) * k)
-                    ag_wait(r, i, way, k)
-
-                    @pl.when((way == 0) | (k < HALF - 1))
-                    def _():
-                        ag_send(r, i, way, k + 1)
+            for i, way, _ in ways(NP):
+                r = wrap(z - (1 - 2 * way) * k)
+                ag_wait(r, i, way, k)
+
+                @pl.when((way == 0) | (k < HALF - 1))
+                def _():
+                    ag_send(r, i, way, k + 1)
             dispatch(list(up_down(k)))
             return carry
         lax.fori_loop(1, HALF, ag_step, 0)
         last = wrap(z + HALF)
-        for i in range(NS):
+        for i in range(NP):
             ag_wait(last, i, 0, HALF)
         dispatch([last])
 
-        arrived(wd_v, r_wd)
+        arrived(wd_v.at[pl.ds(0, NX * UNITS), :], r_twin)
         down_part([z, *up_down(1)])
 
         def late(g, carry):
@@ -554,17 +619,17 @@
         lax.fori_loop(1, HALF // 2, late, 0)
 
         spread = returned([last])
-        chain_first(rs2_in, rs2_out, s_rs2, spread, wd_v)
+        chain_first(rs2_in, rs2_out, s_rs2, slot_b, spread, wd_v)
 
         def rs2_step(s, carry):
-            chain_step(rs2_in, rs2_out, s_rs2, s)
+            chain_step(rs2_in, rs2_out, s_rs2, slot_b, s)
             return carry
         lax.fori_loop(1, HALF, rs2_step, 0)
 
         for t in range(TOK * JX, MSG):
             fin_v[pl.ds(t, DEV, stride=MSG), :] = jnp.zeros((DEV, 128), F32)
         for i, (o, w) in enumerate(SUBS):
-            mixed = chain_end(rs2_in, o, w, i) + hid_v[:, pl.ds(o, w)]
+            mixed = chain_end(rs2_in, slot_b, o, w, i) + hid_v[:, pl.ds(o, w)]
             for t in range(TOK):
                 for j in range(o // 128, (o + w) // 128):
                     fin_v[pl.ds(t * JX + j, DEV, stride=MSG), :] = (
@@ -573,14 +638,18 @@
         for i in range(DEV - 1):
             to = lax.rem(dev + i + 1, DEV)
             send(fin_s.at[to], out_ref.at[x], s_out, r_out, idx(to // NC, z, lax.rem(to, NC)))
-        out_ref[x] = fin_s[dev]
+        out_copy = pltpu.make_async_copy(fin_s.at[dev], out_ref.at[x], l_misc)
+        out_copy.start()
 
         arrived(ctx_v, s_ctx)
         arrived(wo_v.at[pl.ds(0, (NX - 1) * (VH // NC)), :], s_wo)
         arrived(tab_v.at[pl.ds(0, NX - 1)], s_tab)
         arrived(res_v.at[pl.ds(0, NX - 1)], s_res)
         arrived(vu_v.at[pl.ds(0, VH // NC), :], s_core.at[0])
-        arrived(wdn_v, s_core.at[1])
+        @pl.when(half == 1)
+        def _():
+            arrived(wdn_v, s_core.at[1])
+        arrived(wd_v.at[pl.ds(0, NX * UNITS), :], s_wd)
         arrived(wgu_v.at[:, pl.ds(0, UNITS)], s_core.at[2])
         arrived(wgu_v.at[:, pl.ds(0, UNITS)], s_core.at[3])
         for buf, sem in ((rs_out, s_rs), (rs2_out, s_rs2)):
@@ -590,6 +659,8 @@
         arrived(ag_v.at[pl.ds(0, HALF - 1)], s_ag.at[1])
         arrived(dsp_v, s_dsp)
         arrived(fin_s.at[pl.ds(0, DEV - 1)], s_out)
+        arrived(ag_v.at[z, :, pl.ds(DAE, (NX - 1) * BX)], s_bx)
+        out_copy.wait()
         arrived(out_ref.at[pl.ds(0, NX - 1)], r_out)
 
 
@@ -600,11 +671,15 @@
     seqs, steps = resid.shape[:2]
     cache_len = cache_kv.shape[1]
     hbm = pl.BlockSpec(memory_space=pltpu.HBM)
-    vmem = pl.BlockSpec(memory_space=pltpu.VMEM)
-    smem = pl.BlockSpec(memory_space=pltpu.SMEM)
     dma = pltpu.SemaphoreType.DMA
     regular = pltpu.SemaphoreType.REGULAR
     scratch = [
+        pltpu.VMEM(new_kv.shape, BF16),
+        pltpu.SMEM(lengths.shape, jnp.int32),
+        pltpu.VMEM(resid.shape, BF16),
+        pltpu.VMEM((D // 128, 128), BF16),
+        pltpu.SMEM(expert_ids.shape, jnp.int32),
+        pltpu.SMEM(slots.shape, jnp.int32),
         pltpu.VMEM((seqs, KV, cache_len), BF16),
         pltpu.VMEM((seqs, steps * H, KV), BF16),
         pltpu.VMEM((steps * H, cache_len), F32),
@@ -626,9 +701,9 @@
         pltpu.VMEM((DEV * MSG, 128), F32),
         pltpu.VMEM((D // 128, 128), F32),
         pltpu.VMEM((128, DX), BF16),
-        pltpu.VMEM((NZ, ROW, DC), BF16),
-        pltpu.VMEM((NZ, NX, SLOT, DC), BF16),
-        pltpu.VMEM((NZ, NX, SLOT, DC), BF16),
+        pltpu.VMEM((NZ, ROW, DG), BF16),
+        pltpu.VMEM((NZ, NX + 1, SLOT, DAE), BF16),
+        pltpu.VMEM((NZ, NX + 1, SLOT, DAE), BF16),
         pltpu.VMEM((D, 2 * NC * UNITS), BF16),
         pltpu.VMEM((NZ, SLOT, NC * UNITS), BF16),
         pltpu.VMEM((NZ, NX, SLOT, NC * UNITS), BF16),
@@ -639,16 +714,16 @@
         pltpu.VMEM((NZ, ROW, DX), F32),
         pltpu.VMEM((DEV * MSG, 128), F32),
         pltpu.VMEM((DEV, MSG, 128), BF16),
-        dma((seqs,)), dma, dma((3,)),
-        dma, dma, dma, dma, dma((4,)), dma, dma, dma((2,)), dma((2,)), dma((2,)), dma, dma, dma,
-        dma, dma, dma, dma((4,)), dma, dma((NZ,)), dma((2, HALF + 1, NS)), dma,
+        dma((seqs,)), dma, dma((3,)), dma((6,)),
+        dma, dma, dma, dma, dma((4,)), dma, dma, dma((2,)), dma((2,)), dma((2,)), dma, dma, dma, dma,
+        dma, dma, dma, dma((4,)), dma, dma((NZ,)), dma((2, 6, NP)), dma, dma, dma,
         regular, regular,
     ]
     out = pl.pallas_call(
         kernel,
         out_shape=jax.ShapeDtypeStruct((NX, MSG, 128), BF16),
-        in_specs=[hbm, vmem, hbm, smem, vmem, hbm, hbm, vmem, hbm, smem, smem, hbm, hbm, hbm],
-        out_specs=vmem,
+        in_specs=[hbm] * 14,
+        out_specs=hbm,
         scratch_shapes=scratch,
         compiler_params=pltpu.CompilerParams(
             collective_id=0, has_side_effects=True, vmem_limit_bytes=(64 << 20) - (64 << 10)),

time: 123 us -> 120 us (0.976)
  Pallas kernels: 122 us -> 118 us
    pallas_call x1, Pallas kernels: 122 us -> 118 us  [body(): pl.pallas_call(kernel, out_shape=jax.ShapeDtypeStruct((NX, MSG, 128), BF1...]
where the time goes in v3:
time: 120 us
  Pallas kernels  118 us (98%)
  local copies, waits for them, and re-layouts  1.52 us (1%)
    pallas_call x1, Pallas kernels, body(): pl.pallas_call(kernel, out_shape=jax.ShapeDtypeStruct((NX, MSG, 128), BF1...  118 us

profile of v3, /device:TPU:33, one launch (start us, length us, event | category | flops | bytes accessed | tf_op | source)
XLA Modules:
  0.0 119.6 jit_solution(3181844332289186992)
XLA Ops:
  0.0 118.0 %layer.1 = bf16[4,64,128]{2,1,0:T(8,128)(2,1)} custom-call(bf16[2,576,2048]{2,1,0:T(8,128)(2,1)} %bitcast.8, bf16[2,2,576]{2,1,0:T(2,128)(2,1)} %new_h.1, bf16[2,128,576]{2,1,0:T(8,128)(2,1)} %bitcast.9, s32[2]{0:T(128)} %len_h.1, bf16[2,2,7168]{2,1,0:T(2,128)(2,1)} %resid_h.1, bf16[64,512]{1,0:T(8,128)(2,1)} %bitcast.12, bf16[64,7168]{1,0:T(8,128)(2,1)} %wo_h.1, ...), custom_call_target="tpu_custom_call" | custom-call | tf_op jit(solution)/shard_map/layer/pallas_call | solution.py:722
  118.1 0.8 slice.3
  118.9 0.7 reshape.15
  (2 shorter events, 0.0 us)

commit v4 on v3

--- a/solution.py
+++ b/solution.py
@@ -43,12 +43,13 @@
 DA = DX - BX
 DAE = DA + EXT
 DG = DAE + NX * BX
-PIECE = 384
-SUBS = ((DA, BX),) + tuple((o, min(PIECE, DA - o)) for o in range(0, DA, PIECE))
+PIECE = 768
+SUBS = ((DA, BX), (0, 512), (512, 512), (1024, 384))
 NS = len(SUBS)
 NP = DG // PIECE
 NPA = DAE // PIECE
 BLOCKS = ((0, 512), (512, 512), (1024, 768))
+DOWN = 4
 
 F32 = jnp.float32
 BF16 = jnp.bfloat16
@@ -74,12 +75,12 @@
     cache_h, new_h, q_h, len_h, resid_h, vu_h, wo_h, gain_h, router_h, ids_h, slots_h, wg_h, wu_h, wd_h,
     out_ref,
     new_ref, len_ref, resid_ref, gain_ref, ids_ref, slots_ref,
-    cache_v, q_v, score_v, stage_v, ctx_v, arr_v, arrf_v, vu_v, val_v, wo_v, rs_in, rs_out, hid_v, tab_s, tab_v,
+    cache_v, q_v, score_v, stage_v, ctx_v, arr_v, arrf_v, vu_v, val_v, wo_v, ctxn_v, won_v, at_v, rs_in, rs_out, att_v, tab_s, tab_v,
     ress_v, resf_v, res_v, resw_v, gain_v, rout_v, ag_v, dsp_v, d_v, wgu_v, act_s, act_v, wd_v, wdn_v, rs2_in, rs2_out,
-    part_v, fin_v, fin_s,
+    part_v, fin_v, fin_s, sum_v,
     l_cache, l_misc, l_weights, l_small,
     s_ctx, s_tab, s_res, s_wo, s_core, s_wd, s_val, s_rs, s_ag, s_rs2, s_dsp, s_act, s_out, s_bx,
-    r_tab, r_res, r_wo, r_core, r_wd, r_row, r_ring, r_out, r_bx, r_twin,
+    r_tab, r_res, r_wo, r_wox, r_woy, r_core, r_wd, r_row, r_ring, r_out, r_bx, r_twin,
     row_sem, all_sem,
 ):
     me = lax.axis_index("ep")
@@ -136,6 +137,7 @@
     def _():
         for xx in range(NX):
             pl.semaphore_signal(bar, inc=1, device_id=idx(xx, z, 0))
+            pl.semaphore_signal(bar, inc=1, device_id=idx(xx, wrap(z + HALF), 1))
         for step in (1, -1):
             pl.semaphore_signal(bar, inc=1, device_id=idx(x, wrap(z + step), 1))
         pl.semaphore_signal(bar, inc=1, device_id=twin)
@@ -149,19 +151,29 @@
     up_copy = pltpu.make_async_copy(wu_h, wgu_v.at[:, up_at], l_weights.at[2])
     vu_copy = pltpu.make_async_copy(vu_h, vu_v.at[vu_at, :], l_weights.at[0])
 
-    wo_row = pl.ds(mo(x * VH + c * (VH // NC), VH // NC), VH // NC)
+    def wo_rows(xx, cc):
+        return pl.ds(mo(xx * VH + cc * (VH // NC), VH // NC), VH // NC)
 
     def own_columns(xx):
         return pl.ds(mo(xx * DX, 128), DX)
 
-    wo_copy = pltpu.make_async_copy(wo_h.at[:, own_columns(x)], wo_v.at[wo_row, :], l_weights.at[0])
-
-    def wo_send(xx):
-        send(wo_h.at[:, own_columns(xx)], wo_v.at[wo_row, :], s_wo, r_wo, idx(xx, z, 1))
-
     def wd_rows(xx, cc):
         return pl.ds(mo((xx * NC + cc) * UNITS, UNITS), UNITS)
 
+    wo_copy = pltpu.make_async_copy(wo_h.at[:, own_columns(x)], wo_v.at[wo_rows(x, 1), :], l_weights.at[0])
+    wd_copy = pltpu.make_async_copy(wd_h.at[:, own_columns(x)], wd_v.at[wd_rows(x, half), :], l_weights.at[2])
+
+    def wo_send(source):
+        for i in range(NX - 1):
+            xx = xwrap(x + i + 1)
+            send(source.at[:, own_columns(xx)], wo_v.at[wo_rows(x, half), :], s_wo, r_wox.at[i], idx(xx, z, 1))
+
+    def row_next():
+        @pl.when(main & (half == 0))
+        def _():
+            arrived(won_v.at[:, pl.ds(0, (NX - 1) * DX)], r_core.at[2])
+            wo_send(won_v)
+
     def row_start():
         @pl.when(side)
         def _():
@@ -172,11 +184,11 @@
         def _():
             pl.semaphore_wait(row_sem, 1)
 
-        for i in range(NX - 1):
-            wo_send(xwrap(x + i + 1))
-
         @pl.when(main)
         def _():
+            @pl.when(half == 1)
+            def _():
+                wo_send(wo_h)
             wo_copy.start()
             send(vu_h, vu_v.at[vu_at, :], s_core.at[0], r_core.at[0], idx(x, z, 0))
             rout_v[...] = jnp.zeros_like(rout_v)
@@ -184,8 +196,13 @@
 
         @pl.when(side)
         def _():
-            wo_send(x)
             vu_copy.start()
+            @pl.when(half == 0)
+            def _():
+                for i in range(NX - 1):
+                    columns = own_columns(xwrap(x + i + 1))
+                    send(wo_h.at[:, columns], won_v.at[:, columns], s_core.at[0], r_core.at[2], idx(x, z, 1))
+            send(wo_h.at[:, own_columns(x)], wo_v.at[wo_rows(x, 0), :], s_wo, r_wo, idx(x, z, 1))
 
     scale = 1.0 / math.sqrt(QK)
     blk = 512
@@ -194,8 +211,6 @@
     small[0].wait()
     small[1].wait()
     for b in range(2):
-        if b == 1:
-            row_start()
         qb = q_v[b]
         qf = qb.astype(F32)
         step_of = iota((2 * H, 1), 0) // H
@@ -210,6 +225,10 @@
             sc = jnp.where(pos < len_ref[b], sc, -jnp.inf)
             score_v[:, pl.ds(p * blk, blk)] = sc
             peak = jnp.maximum(peak, jnp.max(sc, axis=1, keepdims=True))
+        if b == 0:
+            row_start()
+        else:
+            row_next()
         p_new = [jnp.exp(s - peak) for s in s_new]
         total = p_new[0] + p_new[1]
         acc = p_new[0].astype(BF16).astype(F32) * new_rows[0][:, :LAT]
@@ -226,37 +245,69 @@
 
     @pl.when(main)
     def _():
-        pl.semaphore_wait(bar, NX * NZ + 3)
+        send(ctx_v, ctxn_v, s_ctx.at[0], r_core.at[1], idx(x, z, 0))
+        pl.semaphore_wait(bar, NX * NZ + NX + 3)
         pl.semaphore_signal(all_sem, inc=1, device_id=idx(x, z, 0))
 
     @pl.when(side)
     def _():
+        arrived(ctxn_v, r_core.at[1])
         pl.semaphore_wait(all_sem, 1)
 
+    def near(o):
+        return wrap(jnp.where(lax.rem(o, 2) == 1, z - (o + 1) // 2, z + o // 2))
+
     def ctx_send(o, carry):
-        far = HALF - (o + 1) // 2
-        zz = wrap(jnp.where(lax.rem(o, 2) == 1, z + far, z - far))
+        zz = near(o)
         for i in range(NX):
             xx = xwrap(x + i + 1)
-            own = side & (zz == z) & (xx == x)
-
-            @pl.when(jnp.logical_not(own))
-            def _():
-                send(ctx_v.at[xx * NZ + zz], arr_v.at[z, dev], s_ctx, r_row.at[z], idx(xx, zz, 0))
-
-            @pl.when(own)
-            def _():
-                arr_v[z, dev] = ctx_v[xx * NZ + zz]
+            own = (zz == z) & (xx == x)
+            for core, tiles in ((0, ctx_v), (1, ctxn_v)):
+                @pl.when(jnp.logical_not(own))
+                def _():
+                    send(tiles.at[xx * NZ + zz], arr_v.at[z, x * NC + core], s_ctx.at[core], r_row.at[z],
+                         idx(xx, zz, 0))
+
+                @pl.when(own)
+                def _():
+                    arr_v[z, x * NC + core] = tiles[xx * NZ + zz]
         return carry
-    lax.fori_loop(0, NZ, ctx_send, 0)
+
+    @pl.when(side)
+    def _():
+        lax.fori_loop(0, NZ, ctx_send, 0)
+
+        @pl.when(half == 0)
+        def _():
+            for i in range(NX - 1):
+                columns = own_columns(xwrap(x + i + 1))
+                send(wd_h.at[:, columns], wdn_v.at[:, columns], s_wd.at[0], r_core.at[0], idx(x, z, 1))
+            send(wd_h.at[:, own_columns(x)], wd_v.at[wd_rows(x, half), :], s_wd.at[1], r_wd.at[0], idx(x, z, 1))
 
     @pl.when(main)
     def _():
+        for i in range(NX - 1):
+            xx = xwrap(x + NX - i - 1)
+            view = wo_v.at[wo_rows(xx, half), :]
+            arrived(view, r_wox.at[i])
+            send(view, view, s_wo, r_woy, twin)
+
+        def wd_send(source):
+            for i in range(NX - 1):
+                xx = xwrap(x + i + 1)
+                send(source.at[:, own_columns(xx)], wd_v.at[wd_rows(x, half), :], s_wd.at[0], r_wd.at[1], idx(xx, z, 1))
+
+        @pl.when(half == 0)
+        def _():
+            arrived(wdn_v.at[:, pl.ds(0, (NX - 1) * DX)], r_core.at[0])
+            wd_send(wdn_v)
+
         @pl.when(half == 1)
         def _():
-            send(wd_h, wdn_v, s_core.at[1], r_core.at[1], idx(x, z, 0))
-        send(wg_h, wgu_v.at[:, gate_at], s_core.at[2], r_core.at[2], idx(x, z, 0))
-        send(wu_h, wgu_v.at[:, up_at], s_core.at[3], r_core.at[3], idx(x, z, 0))
+            wd_copy.start()
+            wd_send(wd_h)
+        send(wg_h, wgu_v.at[:, gate_at], s_core.at[1], r_core.at[2], idx(x, z, 0))
+        send(wu_h, wgu_v.at[:, up_at], s_core.at[2], r_core.at[3], idx(x, z, 0))
 
     @pl.when(side)
     def _():
@@ -283,21 +334,61 @@
                 resf_v[pl.ds(xx * MSG + t * JX + j, 1), :] = row[:, col:col + 128]
     ress_v[...] = resf_v[...].reshape(NX, MSG, 128).astype(BF16)
 
-    for xx in range(NX):
-        other = jnp.logical_not(main & (x == xx))
-
-        @pl.when(other)
-        def _():
-            send(tab_s, tab_v.at[dev], s_tab, r_tab, idx(xx, z, 1))
-            send(ress_v.at[xx], res_v.at[dev], s_res, r_res, idx(xx, z, 1))
-
-        @pl.when(jnp.logical_not(other))
-        def _():
-            tab_v[dev] = tab_s[...]
-            res_v[dev] = ress_v[xx]
+    def to_home():
+        for i in range(NX):
+            xx = xwrap(x + i)
+            send(tab_s, tab_v.at[dev], s_tab, r_tab, idx(xx, wrap(z + HALF), 1))
+            send(ress_v.at[xx], res_v.at[dev], s_res, r_res, idx(xx, wrap(z + HALF), 1))
 
     def up_down(k):
         return wrap(z - k), wrap(z + k)
+
+    early = jnp.where(lax.rem(z, CUBE) < CUBE // 2, 1, 0)
+    last = wrap(z + HALF)
+
+    def along(way):
+        return idx(x, wrap(z + 1 - 2 * way), c)
+
+    def ways(pieces):
+        for i in range(pieces + 1):
+            if i < pieces:
+                yield i, early
+            if i > 0:
+                yield i - 1, 1 - early
+
+    def slot_r(s):
+        return lax.rem(s, 3)
+
+    def slot_l(s):
+        return 3 + lax.rem(s, 3)
+
+    def slot_g(k):
+        return lax.rem(k + 2, 3)
+
+    def chain_send(in_ref, out_buf, ssem, slot, way, s, i, total):
+        at = pl.ds(*SUBS[i])
+        out_buf[way, s, :, at] = total.astype(BF16)
+        send(out_buf.at[way, s, :, at], in_ref.at[way, s + 1, :, at], ssem.at[way], r_ring.at[way, slot(s + 1), i],
+             along(way))
+
+    def chain_piece(in_ref, out_buf, ssem, slot, s, i, way):
+        at = pl.ds(*SUBS[i])
+        r = wrap(z - (1 - 2 * way) * s)
+
+        @pl.when((way == 0) | (s >= 2))
+        def _():
+            arrived(in_ref.at[way, s, :, at], r_ring.at[way, slot(s), i])
+        chain_send(in_ref, out_buf, ssem, slot, way, s, i, part_v[r, :, at] + in_ref[way, s, :, at].astype(F32))
+
+    def chain_step(in_ref, out_buf, ssem, slot, s):
+        for i, way in ways(NS):
+            chain_piece(in_ref, out_buf, ssem, slot, s, i, way)
+
+    def chain_end(in_ref, slot, i):
+        at = pl.ds(*SUBS[i])
+        for way in range(2):
+            arrived(in_ref.at[way, HALF, :, at], r_ring.at[way, slot(HALF), i])
+        return part_v[last, :, at] + in_ref[0, HALF, :, at].astype(F32) + in_ref[1, HALF, :, at].astype(F32)
 
     @pl.when(side)
     def _side():
@@ -305,15 +396,10 @@
         arrived(vu_v.at[pl.ds(0, VH // NC), :], r_core.at[0])
         own_lanes = pl.ds(mo(x * VH, VH), VH)
 
-        def wd_send(source):
-            for i in range(NX):
-                xx = xwrap(x + i + 1)
-                send(source.at[:, own_columns(xx)], wd_v.at[wd_rows(x, half), :], s_wd, r_wd, idx(xx, z, 1))
-
         def ctx_row(r):
             @pl.when(r == z)
             def _():
-                arrived(arr_v.at[r, pl.ds(0, DEV - 1)], r_row.at[r])
+                arrived(arr_v.at[r, pl.ds(0, DEV - NC)], r_row.at[r])
 
             @pl.when(r != z)
             def _():
@@ -331,19 +417,10 @@
                 send(view, view, s_val, r_row.at[r], idx(xwrap(x + i + 1), z, 1))
 
         def ctx_step(o, carry):
-            far = HALF - (o + 1) // 2
-            ctx_row(wrap(jnp.where(lax.rem(o, 2) == 1, z + far, z - far)))
+            ctx_row(near(o))
             return carry
         lax.fori_loop(0, NZ, ctx_step, 0)
-
-        @pl.when(half == 0)
-        def _():
-            wd_send(wd_h)
-
-        @pl.when(half == 1)
-        def _():
-            arrived(wdn_v, r_core.at[1])
-            wd_send(wdn_v)
+        to_home()
 
         gate_copy.wait()
         up_copy.wait()
@@ -389,70 +466,48 @@
             experts(list(up_down(k)))
             return carry
         lax.fori_loop(1, HALF, step, 0)
-        experts([wrap(z + HALF)])
-
-        arrived(out_ref, r_out)
-        arrived(ctx_v.at[pl.ds(0, NX * NZ - 1)], s_ctx)
-        arrived(wo_v.at[pl.ds(0, NX * (VH // NC)), :], s_wo)
+        experts([last])
+
+        arrived(ctx_v.at[pl.ds(0, NX * NZ - 1)], s_ctx.at[0])
+        arrived(ctx_v.at[pl.ds(0, NX * NZ - 1)], s_ctx.at[1])
+        @pl.when(half == 0)
+        def _():
+            arrived(won_v.at[:, pl.ds(0, (NX - 1) * DX)], s_core.at[0])
+        arrived(wo_v.at[pl.ds(0, VH // NC), :], s_wo)
         arrived(tab_v.at[pl.ds(0, NX)], s_tab)
         arrived(res_v.at[pl.ds(0, NX)], s_res)
-        arrived(wd_v.at[pl.ds(0, NX * UNITS), :], s_wd)
+
+        @pl.when(half == 0)
+        def _():
+            arrived(wdn_v.at[:, pl.ds(0, (NX - 1) * DX)], s_wd.at[0])
+            arrived(wdn_v.at[:, pl.ds(0, DX)], s_wd.at[1])
         arrived(val_v, s_val)
         arrived(act_v, s_act)
+        arrived(sum_v, r_out)
 
     @pl.when(main)
     def _main():
-        up = idx(x, wrap(z + 1), 1)
         gain_v[...] = gain_ref[...].astype(F32)
-
-        early = jnp.where(lax.rem(z, CUBE) < CUBE // 2, 1, 0)
-
-        def ways(pieces):
-            for i in range(pieces + 1):
-                if i < pieces:
-                    yield i, early, idx(x, wrap(z + 1 - 2 * early), 1)
-                if i > 0:
-                    yield i - 1, 1 - early, idx(x, wrap(z - 1 + 2 * early), 1)
-
-        def slot_a(s):
-            return lax.rem(s, 3)
-
-        def slot_g(k):
-            return lax.rem(k + 2, 3)
-
-        def slot_b(s):
-            return jnp.where(s <= 3, s + 2, lax.rem(s, 3))
-
-        def chain_step(in_ref, out_buf, ssem, slot, s):
-            for i, way, to in ways(NS):
-                at = pl.ds(*SUBS[i])
-                r = wrap(z + (1 - 2 * way) * (HALF - s))
-
-                @pl.when((way == 0) | (s >= 2))
-                def _():
-                    arrived(in_ref.at[way, s, :, at], r_ring.at[way, slot(s), i])
-                total = part_v[r, :, at] + in_ref[way, s, :, at].astype(F32)
-                out_buf[way, s, :, at] = total.astype(BF16)
-                send(out_buf.at[way, s, :, at], in_ref.at[way, s + 1, :, at], ssem.at[way],
-                     r_ring.at[way, slot(s + 1), i], to)
-
-        def chain_first(in_ref, out_buf, ssem, slot, rows, weights):
-            for i, (o, w) in enumerate(SUBS):
-                at = pl.ds(o, w)
-                out_buf[0, 0, :, at] = nn(rows, weights[:, o:o + w]).astype(BF16)
-                send(out_buf.at[0, 0, :, at], in_ref.at[0, 1, :, at], ssem.at[0], r_ring.at[0, slot(1), i], up)
-
-        def chain_end(in_ref, slot, o, w, i):
-            at = pl.ds(o, w)
-            for d in range(2):
-                arrived(in_ref.at[d, HALF, :, at], r_ring.at[d, slot(HALF), i])
-            return part_v[z, :, at] + in_ref[0, HALF, :, at].astype(F32) + in_ref[1, HALF, :, at].astype(F32)
-
         rs_in[1, 1] = jnp.zeros((ROW, DX), BF16)
         rs2_in[1, 1] = jnp.zeros((ROW, DX), BF16)
 
+        def twin_send(xx):
+            view = wd_v.at[wd_rows(xx, half), :]
+            send(view, view, s_wd.at[1], r_twin, twin)
+
+        @pl.when(half == 0)
+        def _():
+            arrived(wd_v.at[wd_rows(x, half), :], r_wd.at[0])
+
+        @pl.when(half == 1)
+        def _():
+            wd_copy.wait()
+        twin_send(x)
+
         wo_copy.wait()
-        arrived(wo_v.at[pl.ds(0, (DEV - 1) * (VH // NC)), :], r_wo)
+        arrived(wo_v.at[wo_rows(x, 0), :], r_wo)
+        arrived(wo_v.at[pl.ds(0, (NX - 1) * (VH // NC)), :], r_woy)
+        to_home()
 
         def attended(rows):
             for r in rows:
@@ -463,29 +518,30 @@
                 for i, r in enumerate(rows):
                     part_v[r, :, pl.ds(o, w)] = part[i * ROW:(i + 1) * ROW]
 
-        first = wrap(z + HALF)
-        arrived(val_v.at[first], r_row.at[first])
-        chain_first(rs_in, rs_out, s_rs, slot_a, val_v[first], wo_v)
-        attended(list(up_down(HALF - 1)))
+        arrived(val_v.at[z], r_row.at[z])
+        for i, (o, w) in enumerate(SUBS):
+            chain_send(rs_in, rs_out, s_rs, slot_r, 0, 0, i, nn(val_v[z], wo_v[:, o:o + w]))
+        attended(list(up_down(1)))
 
         def rs_step(s, carry):
-            chain_step(rs_in, rs_out, s_rs, slot_a, s)
-            ahead = HALF - 1 - s
-
-            @pl.when(ahead >= 1)
-            def _():
-                attended(list(up_down(ahead)))
+            chain_step(rs_in, rs_out, s_rs, slot_r, s)
+
+            @pl.when(s < HALF - 1)
+            def _():
+                attended(list(up_down(s + 1)))
+
+            @pl.when(s == HALF // 2)
+            def _():
+                arrived(wd_v.at[pl.ds(0, (NX - 1) * UNITS), :], r_wd.at[1])
+                for i in range(NX - 1):
+                    twin_send(xwrap(x + i + 1))
             return carry
         lax.fori_loop(1, HALF, rs_step, 0)
-        attended([z])
-
-        arrived(res_v.at[pl.ds(0, DEV - 1)], r_res)
-        arrived(tab_v.at[pl.ds(0, DEV - 1)], r_tab)
+        attended([last])
+
+        arrived(res_v, r_res)
+        arrived(tab_v, r_tab)
         resw_v[...] = res_v[...].reshape(DEV * MSG, 128).astype(F32)
-        for j in range(JX):
-            at = pl.ds(j * 128, 128)
-            part_v[z, :, at] = part_v[z, :, at] + jnp.concatenate(
-                [resw_v[pl.ds(t * JX + j, DEV, stride=MSG), :] for t in range(TOK)], axis=0)
         lane = iota((ROW, 128), 1)
         rows = iota((DEV, 128), 0)
         tabs = []
@@ -499,7 +555,7 @@
 
         def ag_send(r, i, way, k):
             view = ag_v.at[r, :, pl.ds(i * PIECE, PIECE)]
-            send(view, view, s_ag.at[way], r_ring.at[way, slot_g(k), i], idx(x, wrap(z + 1 - 2 * way), 1))
+            send(view, view, s_ag.at[way], r_ring.at[way, slot_g(k), i], along(way))
 
         def ag_wait(r, i, way, k):
             arrived(ag_v.at[r, :, pl.ds(i * PIECE, PIECE)], r_ring.at[way, slot_g(k), i])
@@ -508,7 +564,11 @@
         logits = jnp.zeros((ROW, 128), F32)
         bx_at = pl.ds(mo(DAE + x * BX, 128), BX)
         for i, (o, w) in enumerate(SUBS):
-            hidden = chain_end(rs_in, slot_a, o, w, i)
+            attn = chain_end(rs_in, slot_r, i)
+            att_v[:, pl.ds(o, w)] = attn
+            hidden = attn + jnp.concatenate([
+                jnp.concatenate([resw_v[pl.ds(t * JX + j, DEV, stride=MSG), :] for t in range(TOK)], axis=0)
+                for j in range(o // 128, (o + w) // 128)], axis=1)
             gain = jnp.concatenate(
                 [gain_v[pl.ds(x * JX + j, 1), :] for j in range(o // 128, (o + w) // 128)], axis=1)
             scaled = (hidden * gain).astype(BF16)
@@ -519,10 +579,9 @@
                     send(view, view, s_bx, r_bx, idx(xwrap(x + j + 1), z, 1))
             else:
                 ag_v[z, :, pl.ds(o, w)] = scaled
-                if i < NS - 1:
-                    ag_send(z, i - 1, 0, 1)
-                    ag_send(z, i - 1, 1, 1)
-            hid_v[:, pl.ds(o, w)] = hidden
+                if o + w >= PIECE > o:
+                    ag_send(z, 0, 0, 1)
+                    ag_send(z, 0, 1, 1)
             sums = sums + jnp.sum(hidden * hidden, axis=1, keepdims=True)
             logits = logits + nt(scaled, rout_v[:, pl.ds(o, w)])
         high = logits.astype(BF16).astype(F32)
@@ -533,10 +592,6 @@
         ag_v[z, :, pl.ds(DA, EXT)] = (ext + table_rows).astype(BF16)
         ag_send(z, NPA - 1, 0, 1)
         ag_send(z, NPA - 1, 1, 1)
-        arrived(wd_v.at[pl.ds(0, NX * UNITS), :], r_wd)
-        for xx in range(NX):
-            view = wd_v.at[wd_rows(xx, half), :]
-            send(view, view, s_wd, r_twin, twin)
         arrived(ag_v.at[z, :, pl.ds(DAE, (NX - 1) * BX)], r_bx)
         for i in range(NPA, NP):
             ag_send(z, i, 0, 1)
@@ -560,7 +615,7 @@
                 dsp_v[r, pl.ds(0, NX)] = moved[i * NX * SLOT:(i + 1) * NX * SLOT].reshape(NX, SLOT, DAE)
                 dsp_v[r, NX] = shared[i * SLOT:(i + 1) * SLOT]
             for r in rows:
-                for i in range(1, NX):
+                for i in (2, 1, 3):
                     send(dsp_v.at[r, i], d_v.at[r, x], s_dsp, r_row.at[r], idx(xwrap(x + i), z, 0))
                 send(dsp_v.at[r, 0], d_v.at[r, x], s_dsp, r_row.at[r], idx(x, z, 0))
                 send(dsp_v.at[r, NX], d_v.at[r, NX], s_dsp, r_row.at[r], idx(x, z, 0))
@@ -585,51 +640,92 @@
                 spread.append(nn(place[:, i * n * SLOT:(i + 1) * n * SLOT], acts).astype(BF16))
             return jnp.concatenate(spread, axis=1)
 
+        def down_blocks(rows, blocks):
+            for o, w in blocks:
+                at = pl.ds(o, w)
+                part = nn(at_v[...], wd_v[:, o:o + w])
+                for i, r in enumerate(rows):
+                    part_v[r, :, at] = part[i * ROW:(i + 1) * ROW]
+
         def down_part(rows):
-            spread = returned(rows)
+            at_v[pl.ds(0, len(rows) * ROW), :] = returned(rows)
+            down_blocks(rows, BLOCKS)
+
+        def down_first():
+            spread = returned([z])
             for o, w in BLOCKS:
-                part = nn(spread, wd_v[:, o:o + w])
-                for i, r in enumerate(rows):
-                    part_v[r, :, pl.ds(o, w)] = part[i * ROW:(i + 1) * ROW]
-
+                at = pl.ds(o, w)
+                part_v[z, :, at] = nn(spread, wd_v[:, o:o + w]) + att_v[:, at]
+        at_v[...] = jnp.zeros_like(at_v)
         dispatch([z])
 
         def ag_step(k, carry):
-            for i, way, _ in ways(NP):
-                r = wrap(z - (1 - 2 * way) * k)
-                ag_wait(r, i, way, k)
-
-                @pl.when((way == 0) | (k < HALF - 1))
+            behind = list(up_down(k - 1))
+            done = list(up_down(k - DOWN - 1))
+
+            def pieces(i):
+                for way in (early, 1 - early):
+                    r = wrap(z - (1 - 2 * way) * k)
+                    ag_wait(r, i, way, k)
+
+                    @pl.when((way == 0) | (k < HALF - 1))
+                    def _():
+                        ag_send(r, i, way, k + 1)
+            def follow(i):
+                @pl.when(k > DOWN + 1)
                 def _():
-                    ag_send(r, i, way, k + 1)
-            dispatch(list(up_down(k)))
+                    for way in (early, 1 - early):
+                        chain_piece(rs2_in, rs2_out, s_rs2, slot_l, k - DOWN - 1, i, way)
+            pieces(0)
+
+            @pl.when(k >= 2)
+            def _():
+                dispatch(behind)
+            pieces(1)
+
+            @pl.when(k == DOWN)
+            def _():
+                arrived(wd_v.at[pl.ds(0, NX * UNITS), :], r_twin)
+                down_first()
+
+            @pl.when(k > DOWN + 1)
+            def _():
+                at_v[...] = returned(done)
+                down_blocks(done, BLOCKS[:1])
+            pieces(2)
+
+            @pl.when(k == DOWN + 1)
+            def _():
+                for i, (o, w) in enumerate(SUBS):
+                    chain_send(rs2_in, rs2_out, s_rs2, slot_l, 0, 0, i, part_v[z, :, pl.ds(o, w)])
+
+            @pl.when(k > DOWN + 1)
+            def _():
+                down_blocks(done, BLOCKS[1:])
+            pieces(3)
+            for i in range(NS):
+                follow(i)
             return carry
         lax.fori_loop(1, HALF, ag_step, 0)
-        last = wrap(z + HALF)
+        dispatch(list(up_down(HALF - 1)))
         for i in range(NP):
             ag_wait(last, i, 0, HALF)
         dispatch([last])
 
-        arrived(wd_v.at[pl.ds(0, NX * UNITS), :], r_twin)
-        down_part([z, *up_down(1)])
-
-        def late(g, carry):
-            down_part([*up_down(2 * g), *up_down(2 * g + 1)])
+        down_part(list(up_down(HALF - DOWN - 1)))
+
+        def late(k, carry):
+            chain_step(rs2_in, rs2_out, s_rs2, slot_l, k - 1)
+            down_part(list(up_down(k)))
             return carry
-        lax.fori_loop(1, HALF // 2, late, 0)
-
-        spread = returned([last])
-        chain_first(rs2_in, rs2_out, s_rs2, slot_b, spread, wd_v)
-
-        def rs2_step(s, carry):
-            chain_step(rs2_in, rs2_out, s_rs2, slot_b, s)
-            return carry
-        lax.fori_loop(1, HALF, rs2_step, 0)
+        lax.fori_loop(HALF - DOWN, HALF, late, 0)
+        chain_step(rs2_in, rs2_out, s_rs2, slot_l, HALF - 1)
+        down_part([last])
 
         for t in range(TOK * JX, MSG):
             fin_v[pl.ds(t, DEV, stride=MSG), :] = jnp.zeros((DEV, 128), F32)
         for i, (o, w) in enumerate(SUBS):
-            mixed = chain_end(rs2_in, slot_b, o, w, i) + hid_v[:, pl.ds(o, w)]
+            mixed = chain_end(rs2_in, slot_l, i)
             for t in range(TOK):
                 for j in range(o // 128, (o + w) // 128):
                     fin_v[pl.ds(t * JX + j, DEV, stride=MSG), :] = (
@@ -637,31 +733,32 @@
         fin_s[...] = fin_v[...].reshape(DEV, MSG, 128).astype(BF16)
         for i in range(DEV - 1):
             to = lax.rem(dev + i + 1, DEV)
-            send(fin_s.at[to], out_ref.at[x], s_out, r_out, idx(to // NC, z, lax.rem(to, NC)))
-        out_copy = pltpu.make_async_copy(fin_s.at[dev], out_ref.at[x], l_misc)
-        out_copy.start()
-
-        arrived(ctx_v, s_ctx)
-        arrived(wo_v.at[pl.ds(0, (NX - 1) * (VH // NC)), :], s_wo)
-        arrived(tab_v.at[pl.ds(0, NX - 1)], s_tab)
-        arrived(res_v.at[pl.ds(0, NX - 1)], s_res)
+            send(fin_s.at[to], sum_v.at[x], s_out, r_out, idx(to // NC, z, lax.rem(to, NC)))
+        sum_v[x] = fin_s[dev]
+
+        arrived(ctx_v, s_ctx.at[0])
+        arrived(wo_v.at[pl.ds(0, 2 * (NX - 1) * (VH // NC)), :], s_wo)
+        arrived(tab_v.at[pl.ds(0, NX)], s_tab)
+        arrived(res_v.at[pl.ds(0, NX)], s_res)
         arrived(vu_v.at[pl.ds(0, VH // NC), :], s_core.at[0])
-        @pl.when(half == 1)
-        def _():
-            arrived(wdn_v, s_core.at[1])
-        arrived(wd_v.at[pl.ds(0, NX * UNITS), :], s_wd)
+        arrived(wgu_v.at[:, pl.ds(0, UNITS)], s_core.at[1])
         arrived(wgu_v.at[:, pl.ds(0, UNITS)], s_core.at[2])
-        arrived(wgu_v.at[:, pl.ds(0, UNITS)], s_core.at[3])
-        for buf, sem in ((rs_out, s_rs), (rs2_out, s_rs2)):
-            arrived(buf.at[0], sem.at[0])
-            arrived(buf.at[1, pl.ds(1, HALF - 1)], sem.at[1])
-        arrived(ag_v.at[pl.ds(0, HALF)], s_ag.at[0])
-        arrived(ag_v.at[pl.ds(0, HALF - 1)], s_ag.at[1])
+        arrived(wd_v.at[pl.ds(0, (NX - 1) * UNITS), :], s_wd.at[0])
+        arrived(wd_v.at[pl.ds(0, NX * UNITS), :], s_wd.at[1])
+        for way in range(2):
+            arrived(rs_out.at[way, pl.ds(way, HALF - way)], s_rs.at[way])
+            arrived(rs2_out.at[way, pl.ds(way, HALF - way)], s_rs2.at[way])
+            arrived(ag_v.at[pl.ds(0, HALF - way)], s_ag.at[way])
+        arrived(ag_v.at[z, :, pl.ds(DAE, (NX - 1) * BX)], s_bx)
         arrived(dsp_v, s_dsp)
         arrived(fin_s.at[pl.ds(0, DEV - 1)], s_out)
-        arrived(ag_v.at[z, :, pl.ds(DAE, (NX - 1) * BX)], s_bx)
-        out_copy.wait()
-        arrived(out_ref.at[pl.ds(0, NX - 1)], r_out)
+        arrived(sum_v.at[pl.ds(0, NX - 1)], r_out)
+
+    total = sum_v[...].reshape(NX * MSG, 128).astype(F32) + resf_v[...]
+    ress_v[...] = total.reshape(NX, MSG, 128).astype(BF16)
+    out_copy = pltpu.make_async_copy(ress_v, out_ref, l_misc)
+    out_copy.start()
+    out_copy.wait()
 
 
 def body(
@@ -690,6 +787,9 @@
         pltpu.VMEM((VH, LAT), BF16),
         pltpu.VMEM((NZ, ROW, NX * VH), BF16),
         pltpu.VMEM((NX * VH, DX), BF16),
+        pltpu.VMEM((H, 16, 128), BF16),
+        pltpu.VMEM((VH // NC, D), BF16),
+        pltpu.VMEM((2 * ROW, NX * NC * UNITS), BF16),
         pltpu.VMEM((2, HALF + 1, ROW, DX), BF16),
         pltpu.VMEM((2, HALF, ROW, DX), BF16),
         pltpu.VMEM((ROW, DX), F32),
@@ -714,9 +814,10 @@
         pltpu.VMEM((NZ, ROW, DX), F32),
         pltpu.VMEM((DEV * MSG, 128), F32),
         pltpu.VMEM((DEV, MSG, 128), BF16),
+        pltpu.VMEM((NX, MSG, 128), BF16),
         dma((seqs,)), dma, dma((3,)), dma((6,)),
-        dma, dma, dma, dma, dma((4,)), dma, dma, dma((2,)), dma((2,)), dma((2,)), dma, dma, dma, dma,
-        dma, dma, dma, dma((4,)), dma, dma((NZ,)), dma((2, 6, NP)), dma, dma, dma,
+        dma((2,)), dma, dma, dma, dma((3,)), dma((2,)), dma, dma((2,)), dma((2,)), dma((2,)), dma, dma, dma, dma,
+        dma, dma, dma, dma((3,)), dma, dma((4,)), dma((2,)), dma((NZ,)), dma((2, 6, NP)), dma, dma, dma,
         regular, regular,
     ]
     out = pl.pallas_call(

time: 120 us -> 114 us (0.950)
  Pallas kernels: 118 us -> 113 us
    pallas_call x1, Pallas kernels: 118 us -> 113 us  [body(): pl.pallas_call(kernel, out_shape=jax.ShapeDtypeStruct((NX, MSG, 128), BF1...]
where the time goes in v4:
time: 114 us
  Pallas kernels  113 us (99%)
  local copies, waits for them, and re-layouts  1.52 us (1%)
    pallas_call x1, Pallas kernels, body(): pl.pallas_call(kernel, out_shape=jax.ShapeDtypeStruct((NX, MSG, 128), BF1...  113 us

profile of v4, /device:TPU:33, one launch (start us, length us, event | category | flops | bytes accessed | tf_op | source)
XLA Modules:
  0.0 114.2 jit_solution(6117501926893237326)
XLA Ops:
  0.0 112.7 %layer.1 = bf16[4,64,128]{2,1,0:T(8,128)(2,1)} custom-call(bf16[2,576,2048]{2,1,0:T(8,128)(2,1)} %bitcast.8, bf16[2,2,576]{2,1,0:T(2,128)(2,1)} %new_h.1, bf16[2,128,576]{2,1,0:T(8,128)(2,1)} %bitcast.9, s32[2]{0:T(128)} %len_h.1, bf16[2,2,7168]{2,1,0:T(2,128)(2,1)} %resid_h.1, bf16[64,512]{1,0:T(8,128)(2,1)} %bitcast.12, bf16[64,7168]{1,0:T(8,128)(2,1)} %wo_h.1, ...), custom_call_target="tpu_custom_call" | custom-call | tf_op jit(solution)/shard_map/layer/pallas_call | solution.py:823
  112.7 0.8 slice.3
  113.5 0.7 reshape.15
  (2 shorter events, 0.0 us)

commit v5 on v4

--- a/solution.py
+++ b/solution.py
@@ -30,6 +30,7 @@
 JX = DX // 128
 MSG = 64
 LANE_SUM = 32
+LANE_TOK = 48
 LANE_TAB = 64
 QUAD = EXPERTS // NX
 CHIPS_PER = NZ // QUAD
@@ -75,12 +76,12 @@
     cache_h, new_h, q_h, len_h, resid_h, vu_h, wo_h, gain_h, router_h, ids_h, slots_h, wg_h, wu_h, wd_h,
     out_ref,
     new_ref, len_ref, resid_ref, gain_ref, ids_ref, slots_ref,
-    cache_v, q_v, score_v, stage_v, ctx_v, arr_v, arrf_v, vu_v, val_v, wo_v, ctxn_v, won_v, at_v, rs_in, rs_out, att_v, tab_s, tab_v,
+    cache_v, q_v, score_v, stage_v, ctx_v, arr_v, arrf_v, vu_v, val_v, wo_v, ctxn_v, won_v, rs_in, rs_out, att_v,
     ress_v, resf_v, res_v, resw_v, gain_v, rout_v, ag_v, dsp_v, d_v, wgu_v, act_s, act_v, wd_v, wdn_v, rs2_in, rs2_out,
-    part_v, fin_v, fin_s, sum_v,
+    part_v, fin_v, fin_s, sum_v, outv_v,
     l_cache, l_misc, l_weights, l_small,
-    s_ctx, s_tab, s_res, s_wo, s_core, s_wd, s_val, s_rs, s_ag, s_rs2, s_dsp, s_act, s_out, s_bx,
-    r_tab, r_res, r_wo, r_wox, r_woy, r_core, r_wd, r_row, r_ring, r_out, r_bx, r_twin,
+    s_ctx, s_res, s_wo, s_core, s_wd, s_val, s_rs, s_ag, s_rs2, s_dsp, s_act, s_out, s_bx,
+    r_res, r_wo, r_wox, r_woy, r_core, r_wd, r_row, r_ring, r_out, r_bx, r_twin,
     row_sem, all_sem,
 ):
     me = lax.axis_index("ep")
@@ -163,10 +164,15 @@
     wo_copy = pltpu.make_async_copy(wo_h.at[:, own_columns(x)], wo_v.at[wo_rows(x, 1), :], l_weights.at[0])
     wd_copy = pltpu.make_async_copy(wd_h.at[:, own_columns(x)], wd_v.at[wd_rows(x, half), :], l_weights.at[2])
 
+    def wo_half(xx, h):
+        return pl.ds(mo(xx * DX + h * (DX // 2), 128), DX // 2)
+
     def wo_send(source):
-        for i in range(NX - 1):
-            xx = xwrap(x + i + 1)
-            send(source.at[:, own_columns(xx)], wo_v.at[wo_rows(x, half), :], s_wo, r_wox.at[i], idx(xx, z, 1))
+        for h in range(2):
+            for i in range(NX - 1):
+                xx = xwrap(x + i + 1)
+                send(source.at[:, wo_half(xx, h)], wo_v.at[wo_rows(x, half), wo_half(0, h)], s_wo, r_wox.at[x, h],
+                     idx(xx, z, 1))
 
     def row_next():
         @pl.when(main & (half == 0))
@@ -286,11 +292,12 @@
 
     @pl.when(main)
     def _():
-        for i in range(NX - 1):
-            xx = xwrap(x + NX - i - 1)
-            view = wo_v.at[wo_rows(xx, half), :]
-            arrived(view, r_wox.at[i])
-            send(view, view, s_wo, r_woy, twin)
+        for h in range(2):
+            for i in range(NX - 1):
+                xx = i + jnp.where(x <= i, 1, 0)
+                view = wo_v.at[wo_rows(xx, half), wo_half(0, h)]
+                arrived(view, r_wox.at[xx, h])
+                send(view, view, s_wo, r_woy, twin)
 
         def wd_send(source):
             for i in range(NX - 1):
@@ -318,13 +325,11 @@
         load.wait()
 
     rows8, lanes8 = iota((8, 128), 0), iota((8, 128), 1)
-    table = jnp.zeros((8, 128), F32)
+    table = jnp.where(lanes8 == LANE_TOK, (rows8 + 1).astype(F32), 0.0)
     for t in range(TOK):
         for k in range(TOP):
             hit = (rows8 == t) & (lanes8 == ids_ref[t // 2, t % 2, k] + LANE_TAB)
             table = jnp.where(hit, (slots_ref[t // 2, t % 2, k] + 1).astype(F32), table)
-    tab_s[...] = table
-
     resf_v[...] = jnp.zeros_like(resf_v)
     for t in range(TOK):
         row = resid_ref[t // 2, pl.ds(t % 2, 1), :].astype(F32)
@@ -332,12 +337,13 @@
             for j in range(JX):
                 col = xx * DX + j * 128
                 resf_v[pl.ds(xx * MSG + t * JX + j, 1), :] = row[:, col:col + 128]
+    for xx in range(NX):
+        resf_v[pl.ds(xx * MSG + TOK * JX, 8), :] = table
     ress_v[...] = resf_v[...].reshape(NX, MSG, 128).astype(BF16)
 
     def to_home():
         for i in range(NX):
             xx = xwrap(x + i)
-            send(tab_s, tab_v.at[dev], s_tab, r_tab, idx(xx, wrap(z + HALF), 1))
             send(ress_v.at[xx], res_v.at[dev], s_res, r_res, idx(xx, wrap(z + HALF), 1))
 
     def up_down(k):
@@ -418,6 +424,7 @@
 
         def ctx_step(o, carry):
             ctx_row(near(o))
+
             return carry
         lax.fori_loop(0, NZ, ctx_step, 0)
         to_home()
@@ -428,6 +435,7 @@
         arrived(wgu_v.at[:, pl.ds(0, UNITS)], r_core.at[3])
 
         own_expert = x * QUAD + quad
+        act_at = pl.ds(mo(x * NC * UNITS, 128), NC * UNITS)
 
         def experts(rows):
             for r in rows:
@@ -440,8 +448,15 @@
                     jnp.concatenate([d_v[r, xx, :, pl.ds(0, DA)] for r in rows], axis=0),
                     wgu_v[xx * DX:xx * DX + DA, :])
                 both = both + nn(shared[:, xx * BX:(xx + 1) * BX], wgu_v[xx * DX + DA:(xx + 1) * DX, :])
-                piece = jnp.concatenate([d_v[r, xx, :, pl.ds(DA, EXT)] for r in rows], axis=0).astype(F32)
-                ext = ext + piece
+                piece = jnp.concatenate([d_v[r, xx, :, pl.ds(DA, EXT)] for r in rows], axis=0)
+                ext = ext + piece.astype(F32)
+            n = len(rows)
+            token = nt(jnp.where(iota((n * ROW, 128), 1) == LANE_TOK, 1.0, 0.0).astype(BF16), piece)
+            piece = piece.astype(F32)
+            jj, tok = iota(token.shape, 1), iota(token.shape, 0)
+            wanted = (lax.rem(tok, ROW) // DEV + 1).astype(F32)
+            hit = (token == wanted) & (lax.rem(jj, DEV) == lax.rem(tok, DEV)) & (jj // SLOT == tok // ROW)
+            place = jnp.where(hit, 1.0, 0.0).astype(BF16)
             lane = iota(ext.shape, 1)
             squares = jnp.sum(
                 jnp.where((lane == LANE_SUM) | (lane == LANE_SUM + 1), ext, 0.0), axis=1, keepdims=True)
@@ -455,10 +470,11 @@
             gate = both[:, :NC * UNITS] * inv
             upward = both[:, NC * UNITS:] * inv
             act = (gate / (1.0 + jnp.exp(-gate)) * upward * share).astype(BF16)
+            spread = nn(place, act).astype(BF16)
             for i, r in enumerate(rows):
-                act_s[r] = act[i * SLOT:(i + 1) * SLOT]
-                for n in range(NX):
-                    send(act_s.at[r], act_v.at[r, x], s_act, r_row.at[r], idx(xwrap(x + n + 1), z, 1))
+                act_s[r] = spread[i * ROW:(i + 1) * ROW]
+                for m in range(NX):
+                    send(act_s.at[r], act_v.at[r, :, act_at], s_act, r_row.at[r], idx(xwrap(x + m + 1), z, 1))
 
         experts([z])
 
@@ -474,7 +490,6 @@
         def _():
             arrived(won_v.at[:, pl.ds(0, (NX - 1) * DX)], s_core.at[0])
         arrived(wo_v.at[pl.ds(0, VH // NC), :], s_wo)
-        arrived(tab_v.at[pl.ds(0, NX)], s_tab)
         arrived(res_v.at[pl.ds(0, NX)], s_res)
 
         @pl.when(half == 0)
@@ -540,16 +555,9 @@
         attended([last])
 
         arrived(res_v, r_res)
-        arrived(tab_v, r_tab)
         resw_v[...] = res_v[...].reshape(DEV * MSG, 128).astype(F32)
         lane = iota((ROW, 128), 1)
-        rows = iota((DEV, 128), 0)
-        tabs = []
-        for t in range(TOK):
-            piece = jnp.zeros((DEV, 128), F32)
-            for d in range(DEV):
-                piece = jnp.where(rows == d, tab_v[d, pl.ds(t, 1), :], piece)
-            tabs.append(piece)
+        tabs = [resw_v[pl.ds(TOK * JX + t, DEV, stride=MSG), :] for t in range(TOK)]
         table_rows = jnp.concatenate(tabs, axis=0)
         router_copy.wait()
 
@@ -560,9 +568,9 @@
         def ag_wait(r, i, way, k):
             arrived(ag_v.at[r, :, pl.ds(i * PIECE, PIECE)], r_ring.at[way, slot_g(k), i])
 
+        bx_at = pl.ds(mo(DAE + x * BX, 128), BX)
         sums = jnp.zeros((ROW, 1), F32)
         logits = jnp.zeros((ROW, 128), F32)
-        bx_at = pl.ds(mo(DAE + x * BX, 128), BX)
         for i, (o, w) in enumerate(SUBS):
             attn = chain_end(rs_in, slot_r, i)
             att_v[:, pl.ds(o, w)] = attn
@@ -575,7 +583,7 @@
             if i == 0:
                 ag_v[z, :, bx_at] = scaled
                 view = ag_v.at[z, :, bx_at]
-                for j in range(NX - 1):
+                for j in (1, 0, 2):
                     send(view, view, s_bx, r_bx, idx(xwrap(x + j + 1), z, 1))
             else:
                 ag_v[z, :, pl.ds(o, w)] = scaled
@@ -615,40 +623,24 @@
                 dsp_v[r, pl.ds(0, NX)] = moved[i * NX * SLOT:(i + 1) * NX * SLOT].reshape(NX, SLOT, DAE)
                 dsp_v[r, NX] = shared[i * SLOT:(i + 1) * SLOT]
             for r in rows:
-                for i in (2, 1, 3):
+                for i in (2, 1, 3, 0):
                     send(dsp_v.at[r, i], d_v.at[r, x], s_dsp, r_row.at[r], idx(xwrap(x + i), z, 0))
-                send(dsp_v.at[r, 0], d_v.at[r, x], s_dsp, r_row.at[r], idx(x, z, 0))
                 send(dsp_v.at[r, NX], d_v.at[r, NX], s_dsp, r_row.at[r], idx(x, z, 0))
 
         def returned(rows):
-            n = len(rows)
             for r in rows:
                 arrived(act_v.at[r], r_row.at[r])
-            size = n * NX * SLOT
-            jj, lane = iota((size, 128), 0), iota((size, 128), 1)
-            wanted_lane = LANE_TAB + jj // (n * SLOT) * QUAD + quad
-            pick = jnp.where(lane == wanted_lane, 1.0, 0.0).astype(BF16)
-            picked = nt(jnp.concatenate([ag_v[r, :, pl.ds(DA, EXT)] for r in rows], axis=0), pick)
-            jj, tok = iota((n * ROW, size), 1), iota((n * ROW, size), 0)
-            wanted = (lax.rem(jj, SLOT) // DEV + 1).astype(F32)
-            hit = (picked == wanted) & (lax.rem(jj, DEV) == lax.rem(tok, DEV)) & (
-                lax.rem(jj // SLOT, n) == tok // ROW)
-            place = jnp.where(hit, 1.0, 0.0).astype(BF16)
-            spread = []
-            for i in range(NX):
-                acts = jnp.concatenate([act_v[r, i] for r in rows], axis=0)
-                spread.append(nn(place[:, i * n * SLOT:(i + 1) * n * SLOT], acts).astype(BF16))
-            return jnp.concatenate(spread, axis=1)
+            return jnp.concatenate([act_v[r] for r in rows], axis=0)
 
         def down_blocks(rows, blocks):
             for o, w in blocks:
                 at = pl.ds(o, w)
-                part = nn(at_v[...], wd_v[:, o:o + w])
+                part = nn(jnp.concatenate([act_v[r] for r in rows], axis=0), wd_v[:, o:o + w])
                 for i, r in enumerate(rows):
                     part_v[r, :, at] = part[i * ROW:(i + 1) * ROW]
 
         def down_part(rows):
-            at_v[pl.ds(0, len(rows) * ROW), :] = returned(rows)
+            returned(rows)
             down_blocks(rows, BLOCKS)
 
         def down_first():
@@ -656,7 +648,6 @@
             for o, w in BLOCKS:
                 at = pl.ds(o, w)
                 part_v[z, :, at] = nn(spread, wd_v[:, o:o + w]) + att_v[:, at]
-        at_v[...] = jnp.zeros_like(at_v)
         dispatch([z])
 
         def ag_step(k, carry):
@@ -688,16 +679,16 @@
                 arrived(wd_v.at[pl.ds(0, NX * UNITS), :], r_twin)
                 down_first()
 
+            @pl.when(k == DOWN + 1)
+            def _():
+                for i, (o, w) in enumerate(SUBS):
+                    chain_send(rs2_in, rs2_out, s_rs2, slot_l, 0, 0, i, part_v[z, :, pl.ds(o, w)])
+
             @pl.when(k > DOWN + 1)
             def _():
-                at_v[...] = returned(done)
+                returned(done)
                 down_blocks(done, BLOCKS[:1])
             pieces(2)
-
-            @pl.when(k == DOWN + 1)
-            def _():
-                for i, (o, w) in enumerate(SUBS):
-                    chain_send(rs2_in, rs2_out, s_rs2, slot_l, 0, 0, i, part_v[z, :, pl.ds(o, w)])
 
             @pl.when(k > DOWN + 1)
             def _():
@@ -738,7 +729,6 @@
 
         arrived(ctx_v, s_ctx.at[0])
         arrived(wo_v.at[pl.ds(0, 2 * (NX - 1) * (VH // NC)), :], s_wo)
-        arrived(tab_v.at[pl.ds(0, NX)], s_tab)
         arrived(res_v.at[pl.ds(0, NX)], s_res)
         arrived(vu_v.at[pl.ds(0, VH // NC), :], s_core.at[0])
         arrived(wgu_v.at[:, pl.ds(0, UNITS)], s_core.at[1])
@@ -754,9 +744,11 @@
         arrived(fin_s.at[pl.ds(0, DEV - 1)], s_out)
         arrived(sum_v.at[pl.ds(0, NX - 1)], r_out)
 
-    total = sum_v[...].reshape(NX * MSG, 128).astype(F32) + resf_v[...]
-    ress_v[...] = total.reshape(NX, MSG, 128).astype(BF16)
-    out_copy = pltpu.make_async_copy(ress_v, out_ref, l_misc)
+    resf_v[...] = sum_v[...].reshape(NX * MSG, 128).astype(F32) + resf_v[...]
+    for t in range(TOK):
+        rows = [resf_v[pl.ds(xx * MSG + t * JX, JX), :] for xx in range(NX)]
+        outv_v[t] = jnp.concatenate(rows, axis=0).astype(BF16)
+    out_copy = pltpu.make_async_copy(outv_v, out_ref, l_misc)
     out_copy.start()
     out_copy.wait()
 
@@ -789,12 +781,9 @@
         pltpu.VMEM((NX * VH, DX), BF16),
         pltpu.VMEM((H, 16, 128), BF16),
         pltpu.VMEM((VH // NC, D), BF16),
-        pltpu.VMEM((2 * ROW, NX * NC * UNITS), BF16),
         pltpu.VMEM((2, HALF + 1, ROW, DX), BF16),
         pltpu.VMEM((2, HALF, ROW, DX), BF16),
         pltpu.VMEM((ROW, DX), F32),
-        pltpu.VMEM((8, 128), F32),
-        pltpu.VMEM((DEV, 8, 128), F32),
         pltpu.VMEM((NX, MSG, 128), BF16),
         pltpu.VMEM((NX * MSG, 128), F32),
         pltpu.VMEM((DEV, MSG, 128), BF16),
@@ -805,8 +794,8 @@
         pltpu.VMEM((NZ, NX + 1, SLOT, DAE), BF16),
         pltpu.VMEM((NZ, NX + 1, SLOT, DAE), BF16),
         pltpu.VMEM((D, 2 * NC * UNITS), BF16),
-        pltpu.VMEM((NZ, SLOT, NC * UNITS), BF16),
-        pltpu.VMEM((NZ, NX, SLOT, NC * UNITS), BF16),
+        pltpu.VMEM((NZ, ROW, NC * UNITS), BF16),
+        pltpu.VMEM((NZ, ROW, NX * NC * UNITS), BF16),
         pltpu.VMEM((NX * NC * UNITS, DX), BF16),
         pltpu.VMEM((UNITS, D), BF16),
         pltpu.VMEM((2, HALF + 1, ROW, DX), BF16),
@@ -815,14 +804,15 @@
         pltpu.VMEM((DEV * MSG, 128), F32),
         pltpu.VMEM((DEV, MSG, 128), BF16),
         pltpu.VMEM((NX, MSG, 128), BF16),
+        pltpu.VMEM((TOK, NX * JX, 128), BF16),
         dma((seqs,)), dma, dma((3,)), dma((6,)),
-        dma((2,)), dma, dma, dma, dma((3,)), dma((2,)), dma, dma((2,)), dma((2,)), dma((2,)), dma, dma, dma, dma,
-        dma, dma, dma, dma((3,)), dma, dma((4,)), dma((2,)), dma((NZ,)), dma((2, 6, NP)), dma, dma, dma,
+        dma((2,)), dma, dma, dma((3,)), dma((2,)), dma, dma((2,)), dma((2,)), dma((2,)), dma, dma, dma, dma,
+        dma, dma, dma((NX, 2)), dma, dma((4,)), dma((2,)), dma((NZ,)), dma((2, 6, NP)), dma, dma, dma,
         regular, regular,
     ]
     out = pl.pallas_call(
         kernel,
-        out_shape=jax.ShapeDtypeStruct((NX, MSG, 128), BF16),
+        out_shape=jax.ShapeDtypeStruct((TOK, NX * JX, 128), BF16),
         in_specs=[hbm] * 14,
         out_specs=hbm,
         scratch_shapes=scratch,
@@ -833,7 +823,6 @@
         jnp.transpose(cache_kv, (0, 2, 1)), new_kv, queries.reshape(seqs, steps * H, KV), lengths, resid,
         value_up.T, out_proj, norm_gain.reshape(D // 128, 128), router.T, expert_ids, slots, w_gate, w_up, w_down,
     )
-    out = out[:, :TOK * JX].reshape(NX, TOK, JX, 128).transpose(1, 0, 2, 3)
     return out.reshape(resid.shape)
 
 

time: 114 us -> 112 us (0.982)
  Pallas kernels: 113 us -> 111 us
    pallas_call x1, Pallas kernels: 113 us -> 111 us  [body(): pl.pallas_call(kernel, out_shape=jax.ShapeDtypeStruct((TOK, NX * JX, 128)...]
where the time goes in v5:
time: 112 us
  Pallas kernels  111 us (99%)
  local copies, waits for them, and re-layouts  1.46 us (1%)
    pallas_call x1, Pallas kernels, body(): pl.pallas_call(kernel, out_shape=jax.ShapeDtypeStruct((TOK, NX * JX, 128)...  111 us

profile of v5, /device:TPU:33, one launch (start us, length us, event | category | flops | bytes accessed | tf_op | source)
XLA Modules:
  0.0 112.0 jit_solution(6229610664886415385)
XLA Ops:
  0.0 110.6 %layer.1 = bf16[4,56,128]{2,1,0:T(8,128)(2,1)} custom-call(bf16[2,576,2048]{2,1,0:T(8,128)(2,1)} %bitcast.5, bf16[2,2,576]{2,1,0:T(2,128)(2,1)} %new_h.1, bf16[2,128,576]{2,1,0:T(8,128)(2,1)} %bitcast.6, s32[2]{0:T(128)} %len_h.1, bf16[2,2,7168]{2,1,0:T(2,128)(2,1)} %resid_h.1, bf16[64,512]{1,0:T(8,128)(2,1)} %bitcast.8, bf16[64,7168]{1,0:T(8,128)(2,1)} %wo_h.1, ...), custom_call_target="tpu_custom_call" | custom-call | tf_op jit(solution)/shard_map/layer/pallas_call | solution.py:813
  110.6 1.5 %reshape.11 = bf16[2,2,7168]{2,1,0:T(2,128)(2,1)} reshape(bf16[4,56,128]{2,1,0:T(8,128)(2,1)} %layer.1) | data formatting | bytes 114688 | tf_op jit(solution)/shard_map/reshape | solution.py:826

commit v6 on v5

--- a/solution.py
+++ b/solution.py
@@ -45,7 +45,7 @@
 DAE = DA + EXT
 DG = DAE + NX * BX
 PIECE = 768
-SUBS = ((DA, BX), (0, 512), (512, 512), (1024, 384))
+SUBS = ((DA, BX), (0, 256), (256, 256), (512, 256), (768, 256), (1024, 384))
 NS = len(SUBS)
 NP = DG // PIECE
 NPA = DAE // PIECE
@@ -587,9 +587,10 @@
                     send(view, view, s_bx, r_bx, idx(xwrap(x + j + 1), z, 1))
             else:
                 ag_v[z, :, pl.ds(o, w)] = scaled
-                if o + w >= PIECE > o:
-                    ag_send(z, 0, 0, 1)
-                    ag_send(z, 0, 1, 1)
+                for piece in range(NPA - 1):
+                    if o < (piece + 1) * PIECE <= o + w:
+                        ag_send(z, piece, 0, 1)
+                        ag_send(z, piece, 1, 1)
             sums = sums + jnp.sum(hidden * hidden, axis=1, keepdims=True)
             logits = logits + nt(scaled, rout_v[:, pl.ds(o, w)])
         high = logits.astype(BF16).astype(F32)
@@ -807,7 +808,7 @@
         pltpu.VMEM((TOK, NX * JX, 128), BF16),
         dma((seqs,)), dma, dma((3,)), dma((6,)),
         dma((2,)), dma, dma, dma((3,)), dma((2,)), dma, dma((2,)), dma((2,)), dma((2,)), dma, dma, dma, dma,
-        dma, dma, dma((NX, 2)), dma, dma((4,)), dma((2,)), dma((NZ,)), dma((2, 6, NP)), dma, dma, dma,
+        dma, dma, dma((NX, 2)), dma, dma((4,)), dma((2,)), dma((NZ,)), dma((2, 6, max(NP, NS))), dma, dma, dma,
         regular, regular,
     ]
     out = pl.pallas_call(

time: 112 us -> 112 us (level)
  no operation moved by 1% of the time
where the time goes in v6:
time: 112 us; the launch traced here: 111 us
  Pallas kernels  110 us (98%)
  local copies, waits for them, and re-layouts  1.46 us (1%)
    pallas_call x1, Pallas kernels, body(): pl.pallas_call(kernel, out_shape=jax.ShapeDtypeStruct((TOK, NX * JX, 128)...  110 us

profile of v6, /device:TPU:33, one launch (start us, length us, event | category | flops | bytes accessed | tf_op | source)
XLA Modules:
  0.0 111.3 jit_solution(4322761550958728515)
XLA Ops:
  0.0 109.9 %layer.1 = bf16[4,56,128]{2,1,0:T(8,128)(2,1)} custom-call(bf16[2,576,2048]{2,1,0:T(8,128)(2,1)} %bitcast.5, bf16[2,2,576]{2,1,0:T(2,128)(2,1)} %new_h.1, bf16[2,128,576]{2,1,0:T(8,128)(2,1)} %bitcast.6, s32[2]{0:T(128)} %len_h.1, bf16[2,2,7168]{2,1,0:T(2,128)(2,1)} %resid_h.1, bf16[64,512]{1,0:T(8,128)(2,1)} %bitcast.8, bf16[64,7168]{1,0:T(8,128)(2,1)} %wo_h.1, ...), custom_call_target="tpu_custom_call" | custom-call | tf_op jit(solution)/shard_map/layer/pallas_call | solution.py:814
  109.9 1.5 %reshape.11 = bf16[2,2,7168]{2,1,0:T(2,128)(2,1)} reshape(bf16[4,56,128]{2,1,0:T(8,128)(2,1)} %layer.1) | data formatting | bytes 114688 | tf_op jit(solution)/shard_map/reshape | solution.py:827

commit v7 on v6

--- a/solution.py
+++ b/solution.py
@@ -40,15 +40,15 @@
 
 CUBE = 4
 
-BX = 384
+BX = 128
 DA = DX - BX
 DAE = DA + EXT
 DG = DAE + NX * BX
-PIECE = 768
-SUBS = ((DA, BX), (0, 256), (256, 256), (512, 256), (768, 256), (1024, 384))
+PIECES = ((0, 640), (640, 512), (1152, 640), (1792, 512))
+SUBS = ((DA, BX), (0, 256), (256, 256), (512, 256), (768, 256), (1024, 256), (1280, 384))
 NS = len(SUBS)
-NP = DG // PIECE
-NPA = DAE // PIECE
+NP = len(PIECES)
+NPA = sum(o < DAE for o, _ in PIECES)
 BLOCKS = ((0, 512), (512, 512), (1024, 768))
 DOWN = 4
 
@@ -77,10 +77,10 @@
     out_ref,
     new_ref, len_ref, resid_ref, gain_ref, ids_ref, slots_ref,
     cache_v, q_v, score_v, stage_v, ctx_v, arr_v, arrf_v, vu_v, val_v, wo_v, ctxn_v, won_v, rs_in, rs_out, att_v,
-    ress_v, resf_v, res_v, resw_v, gain_v, rout_v, ag_v, dsp_v, d_v, wgu_v, act_s, act_v, wd_v, wdn_v, rs2_in, rs2_out,
+    ress_v, resf_v, res_v, resw_v, gain_v, rout_v, ag_v, dsp_v, shr_v, d_v, wgu_v, act_s, act_v, wd_v, wdn_v, rs2_in, rs2_out,
     part_v, fin_v, fin_s, sum_v, outv_v,
     l_cache, l_misc, l_weights, l_small,
-    s_ctx, s_res, s_wo, s_core, s_wd, s_val, s_rs, s_ag, s_rs2, s_dsp, s_act, s_out, s_bx,
+    s_ctx, s_res, s_wo, s_core, s_wd, s_val, s_rs, s_ag, s_rs2, s_dsp, s_act, s_out, s_bx, s_shr,
     r_res, r_wo, r_wox, r_woy, r_core, r_wd, r_row, r_ring, r_out, r_bx, r_twin,
     row_sem, all_sem,
 ):
@@ -442,13 +442,13 @@
                 arrived(d_v.at[r], r_row.at[r])
             both = jnp.zeros((SLOT * len(rows), 2 * NC * UNITS), F32)
             ext = jnp.zeros((SLOT * len(rows), EXT), F32)
-            shared = jnp.concatenate([d_v[r, NX] for r in rows], axis=0)
+            shared = jnp.concatenate([d_v[r, :, pl.ds(NX * DAE, NX * BX)] for r in rows], axis=0)
             for xx in range(NX):
                 both = both + nn(
-                    jnp.concatenate([d_v[r, xx, :, pl.ds(0, DA)] for r in rows], axis=0),
+                    jnp.concatenate([d_v[r, :, pl.ds(xx * DAE, DA)] for r in rows], axis=0),
                     wgu_v[xx * DX:xx * DX + DA, :])
                 both = both + nn(shared[:, xx * BX:(xx + 1) * BX], wgu_v[xx * DX + DA:(xx + 1) * DX, :])
-                piece = jnp.concatenate([d_v[r, xx, :, pl.ds(DA, EXT)] for r in rows], axis=0)
+                piece = jnp.concatenate([d_v[r, :, pl.ds(xx * DAE + DA, EXT)] for r in rows], axis=0)
                 ext = ext + piece.astype(F32)
             n = len(rows)
             token = nt(jnp.where(iota((n * ROW, 128), 1) == LANE_TOK, 1.0, 0.0).astype(BF16), piece)
@@ -562,11 +562,11 @@
         router_copy.wait()
 
         def ag_send(r, i, way, k):
-            view = ag_v.at[r, :, pl.ds(i * PIECE, PIECE)]
+            view = ag_v.at[r, :, pl.ds(*PIECES[i])]
             send(view, view, s_ag.at[way], r_ring.at[way, slot_g(k), i], along(way))
 
         def ag_wait(r, i, way, k):
-            arrived(ag_v.at[r, :, pl.ds(i * PIECE, PIECE)], r_ring.at[way, slot_g(k), i])
+            arrived(ag_v.at[r, :, pl.ds(*PIECES[i])], r_ring.at[way, slot_g(k), i])
 
         bx_at = pl.ds(mo(DAE + x * BX, 128), BX)
         sums = jnp.zeros((ROW, 1), F32)
@@ -587,8 +587,8 @@
                     send(view, view, s_bx, r_bx, idx(xwrap(x + j + 1), z, 1))
             else:
                 ag_v[z, :, pl.ds(o, w)] = scaled
-                for piece in range(NPA - 1):
-                    if o < (piece + 1) * PIECE <= o + w:
+                for piece, (start, size) in enumerate(PIECES[:NPA - 1]):
+                    if o < start + size <= o + w:
                         ag_send(z, piece, 0, 1)
                         ag_send(z, piece, 1, 1)
             sums = sums + jnp.sum(hidden * hidden, axis=1, keepdims=True)
@@ -606,6 +606,8 @@
             ag_send(z, i, 0, 1)
             ag_send(z, i, 1, 1)
 
+        d_at = pl.ds(mo(x * DAE, 128), DAE)
+
         def dispatch(rows):
             n = len(rows)
             size = n * NX * SLOT
@@ -621,12 +623,12 @@
             own = jnp.concatenate([place[i * NX * SLOT:i * NX * SLOT + SLOT] for i in range(n)], axis=0)
             shared = nn(own, jnp.concatenate([ag_v[r, :, pl.ds(DAE, NX * BX)] for r in rows], axis=0)).astype(BF16)
             for i, r in enumerate(rows):
-                dsp_v[r, pl.ds(0, NX)] = moved[i * NX * SLOT:(i + 1) * NX * SLOT].reshape(NX, SLOT, DAE)
-                dsp_v[r, NX] = shared[i * SLOT:(i + 1) * SLOT]
+                dsp_v[r] = moved[i * NX * SLOT:(i + 1) * NX * SLOT].reshape(NX, SLOT, DAE)
+                shr_v[r] = shared[i * SLOT:(i + 1) * SLOT]
             for r in rows:
                 for i in (2, 1, 3, 0):
-                    send(dsp_v.at[r, i], d_v.at[r, x], s_dsp, r_row.at[r], idx(xwrap(x + i), z, 0))
-                send(dsp_v.at[r, NX], d_v.at[r, NX], s_dsp, r_row.at[r], idx(x, z, 0))
+                    send(dsp_v.at[r, i], d_v.at[r, :, d_at], s_dsp, r_row.at[r], idx(xwrap(x + i), z, 0))
+                send(shr_v.at[r], d_v.at[r, :, pl.ds(NX * DAE, NX * BX)], s_shr, r_row.at[r], idx(x, z, 0))
 
         def returned(rows):
             for r in rows:
@@ -742,6 +744,7 @@
             arrived(ag_v.at[pl.ds(0, HALF - way)], s_ag.at[way])
         arrived(ag_v.at[z, :, pl.ds(DAE, (NX - 1) * BX)], s_bx)
         arrived(dsp_v, s_dsp)
+        arrived(shr_v, s_shr)
         arrived(fin_s.at[pl.ds(0, DEV - 1)], s_out)
         arrived(sum_v.at[pl.ds(0, NX - 1)], r_out)
 
@@ -792,8 +795,9 @@
         pltpu.VMEM((D // 128, 128), F32),
         pltpu.VMEM((128, DX), BF16),
         pltpu.VMEM((NZ, ROW, DG), BF16),
-        pltpu.VMEM((NZ, NX + 1, SLOT, DAE), BF16),
-        pltpu.VMEM((NZ, NX + 1, SLOT, DAE), BF16),
+        pltpu.VMEM((NZ, NX, SLOT, DAE), BF16),
+        pltpu.VMEM((NZ, SLOT, NX * BX), BF16),
+        pltpu.VMEM((NZ, SLOT, NX * (DAE + BX)), BF16),
         pltpu.VMEM((D, 2 * NC * UNITS), BF16),
         pltpu.VMEM((NZ, ROW, NC * UNITS), BF16),
         pltpu.VMEM((NZ, ROW, NX * NC * UNITS), BF16),
@@ -807,7 +811,7 @@
         pltpu.VMEM((NX, MSG, 128), BF16),
         pltpu.VMEM((TOK, NX * JX, 128), BF16),
         dma((seqs,)), dma, dma((3,)), dma((6,)),
-        dma((2,)), dma, dma, dma((3,)), dma((2,)), dma, dma((2,)), dma((2,)), dma((2,)), dma, dma, dma, dma,
+        dma((2,)), dma, dma, dma((3,)), dma((2,)), dma, dma((2,)), dma((2,)), dma((2,)), dma, dma, dma, dma, dma,
         dma, dma, dma((NX, 2)), dma, dma((4,)), dma((2,)), dma((NZ,)), dma((2, 6, max(NP, NS))), dma, dma, dma,
         regular, regular,
     ]

time: 112 us -> 111 us (level)
  no operation moved by 1% of the time
where the time goes in v7:
time: 111 us
  Pallas kernels  109 us (98%)
  local copies, waits for them, and re-layouts  1.46 us (1%)
    pallas_call x1, Pallas kernels, body(): pl.pallas_call(kernel, out_shape=jax.ShapeDtypeStruct((TOK, NX * JX, 128)...  109 us

profile of v7, /device:TPU:33, one launch (start us, length us, event | category | flops | bytes accessed | tf_op | source)
XLA Modules:
  0.0 110.5 jit_solution(3490612990901009960)
XLA Ops:
  0.0 109.0 %layer.1 = bf16[4,56,128]{2,1,0:T(8,128)(2,1)} custom-call(bf16[2,576,2048]{2,1,0:T(8,128)(2,1)} %bitcast.5, bf16[2,2,576]{2,1,0:T(2,128)(2,1)} %new_h.1, bf16[2,128,576]{2,1,0:T(8,128)(2,1)} %bitcast.6, s32[2]{0:T(128)} %len_h.1, bf16[2,2,7168]{2,1,0:T(2,128)(2,1)} %resid_h.1, bf16[64,512]{1,0:T(8,128)(2,1)} %bitcast.8, bf16[64,7168]{1,0:T(8,128)(2,1)} %wo_h.1, ...), custom_call_target="tpu_custom_call" | custom-call | tf_op jit(solution)/shard_map/layer/pallas_call | solution.py:818
  109.0 1.5 %reshape.11 = bf16[2,2,7168]{2,1,0:T(2,128)(2,1)} reshape(bf16[4,56,128]{2,1,0:T(8,128)(2,1)} %layer.1) | data formatting | bytes 114688 | tf_op jit(solution)/shard_map/reshape | solution.py:831

commit v8 on v7

--- a/solution.py
+++ b/solution.py
@@ -696,9 +696,9 @@
             @pl.when(k > DOWN + 1)
             def _():
                 down_blocks(done, BLOCKS[1:])
-            pieces(3)
             for i in range(NS):
                 follow(i)
+            pieces(3)
             return carry
         lax.fori_loop(1, HALF, ag_step, 0)
         dispatch(list(up_down(HALF - 1)))

time: 111 us -> 111 us (level)
  no operation moved by 1% of the time
where the time goes in v8:
time: 111 us
  Pallas kernels  109 us (98%)
  local copies, waits for them, and re-layouts  1.46 us (1%)
    pallas_call x1, Pallas kernels, body(): pl.pallas_call(kernel, out_shape=jax.ShapeDtypeStruct((TOK, NX * JX, 128)...  109 us

profile of v8, /device:TPU:33, one launch (start us, length us, event | category | flops | bytes accessed | tf_op | source)
XLA Modules:
  0.0 110.5 jit_solution(8624096033785260767)
XLA Ops:
  0.0 109.0 %layer.1 = bf16[4,56,128]{2,1,0:T(8,128)(2,1)} custom-call(bf16[2,576,2048]{2,1,0:T(8,128)(2,1)} %bitcast.5, bf16[2,2,576]{2,1,0:T(2,128)(2,1)} %new_h.1, bf16[2,128,576]{2,1,0:T(8,128)(2,1)} %bitcast.6, s32[2]{0:T(128)} %len_h.1, bf16[2,2,7168]{2,1,0:T(2,128)(2,1)} %resid_h.1, bf16[64,512]{1,0:T(8,128)(2,1)} %bitcast.8, bf16[64,7168]{1,0:T(8,128)(2,1)} %wo_h.1, ...), custom_call_target="tpu_custom_call" | custom-call | tf_op jit(solution)/shard_map/layer/pallas_call | solution.py:818
  109.0 1.5 %reshape.11 = bf16[2,2,7168]{2,1,0:T(2,128)(2,1)} reshape(bf16[4,56,128]{2,1,0:T(8,128)(2,1)} %layer.1) | data formatting | bytes 114688 | tf_op jit(solution)/shard_map/reshape | solution.py:831

commit v9 on v8

--- a/solution.py
+++ b/solution.py
@@ -419,8 +419,8 @@
             rows = jnp.concatenate(cols, axis=1).astype(BF16)
             val_v[r, :, own_lanes] = nt(rows, vu_v[...]).astype(BF16)
             view = val_v.at[r, :, own_lanes]
-            for i in range(NX):
-                send(view, view, s_val, r_row.at[r], idx(xwrap(x + i + 1), z, 1))
+            for i in (2, 1, 3, 0):
+                send(view, view, s_val, r_row.at[r], idx(xwrap(x + i), z, 1))
 
         def ctx_step(o, carry):
             ctx_row(near(o))
@@ -473,8 +473,8 @@
             spread = nn(place, act).astype(BF16)
             for i, r in enumerate(rows):
                 act_s[r] = spread[i * ROW:(i + 1) * ROW]
-                for m in range(NX):
-                    send(act_s.at[r], act_v.at[r, :, act_at], s_act, r_row.at[r], idx(xwrap(x + m + 1), z, 1))
+                for m in (2, 1, 3, 0):
+                    send(act_s.at[r], act_v.at[r, :, act_at], s_act, r_row.at[r], idx(xwrap(x + m), z, 1))
 
         experts([z])
 
@@ -725,8 +725,8 @@
                     fin_v[pl.ds(t * JX + j, DEV, stride=MSG), :] = (
                         mixed[t * DEV:(t + 1) * DEV, j * 128 - o:j * 128 - o + 128])
         fin_s[...] = fin_v[...].reshape(DEV, MSG, 128).astype(BF16)
-        for i in range(DEV - 1):
-            to = lax.rem(dev + i + 1, DEV)
+        for i in (4, 3, 5, 2, 6, 1, 7):
+            to = lax.rem(dev + i, DEV)
             send(fin_s.at[to], sum_v.at[x], s_out, r_out, idx(to // NC, z, lax.rem(to, NC)))
         sum_v[x] = fin_s[dev]
 

time: 111 us -> 110 us (level)
  no operation moved by 1% of the time
where the time goes in v9:
time: 110 us
  Pallas kernels  109 us (99%)
  local copies, waits for them, and re-layouts  1.46 us (1%)
    pallas_call x1, Pallas kernels, body(): pl.pallas_call(kernel, out_shape=jax.ShapeDtypeStruct((TOK, NX * JX, 128)...  109 us

profile of v9, /device:TPU:33, one launch (start us, length us, event | category | flops | bytes accessed | tf_op | source)
XLA Modules:
  0.0 110.3 jit_solution(13174197900694762495)
XLA Ops:
  0.0 108.8 %layer.1 = bf16[4,56,128]{2,1,0:T(8,128)(2,1)} custom-call(bf16[2,576,2048]{2,1,0:T(8,128)(2,1)} %bitcast.5, bf16[2,2,576]{2,1,0:T(2,128)(2,1)} %new_h.1, bf16[2,128,576]{2,1,0:T(8,128)(2,1)} %bitcast.6, s32[2]{0:T(128)} %len_h.1, bf16[2,2,7168]{2,1,0:T(2,128)(2,1)} %resid_h.1, bf16[64,512]{1,0:T(8,128)(2,1)} %bitcast.8, bf16[64,7168]{1,0:T(8,128)(2,1)} %wo_h.1, ...), custom_call_target="tpu_custom_call" | custom-call | tf_op jit(solution)/shard_map/layer/pallas_call | solution.py:818
  108.8 1.5 %reshape.11 = bf16[2,2,7168]{2,1,0:T(2,128)(2,1)} reshape(bf16[4,56,128]{2,1,0:T(8,128)(2,1)} %layer.1) | data formatting | bytes 114688 | tf_op jit(solution)/shard_map/reshape | solution.py:831
